TPU v7x, 32 devices: a whole 2x2x4 slice. The times are simulated.
32 devices in a mesh: dp: 2 (over x), tp: 4 (over z), section: 4 (over y, core).
Axes of the slice: x: 2, y: 2, z: 4, core: 2. Of those that a mesh axis runs over, the one named last changes fastest.
Arguments:
- tokens: bfloat16 [256, 2304], P('dp', 'section'), may hold values from -6 to 6
- hidden_grad: bfloat16 [256, 18432], P('dp', ('tp', 'section')), may hold values from -6 to 6
- norm_gain: float32 [2304], replicated, may hold values from 0.5 to 1.5
- w_gate: bfloat16 [2304, 18432], P('dp', ('tp', 'section')), may hold values from -0.125 to 0.125
- w_up: bfloat16 [2304, 18432], P('dp', ('tp', 'section')), may hold values from -0.125 to 0.125
Outputs:
- grad_tokens: bfloat16 [256, 2304], P('dp', ('tp', 'section'))
- grad_gain: float32 [2304], P(('tp', 'section'))
- grad_gate: bfloat16 [2304, 18432], P('dp', ('tp', 'section'))
- grad_up: bfloat16 [2304, 18432], P('dp', ('tp', 'section'))
All inputs are finite; a program needn't handle non-finite values.
Results may differ from a plain program's by a relative error of at most 0.018.
Values may be sent and summed in bfloat16 or wider, within the bound.
A program may use at most 128 MiB of HBM per device.

v0:
```python
import functools

import jax
import jax.numpy as jnp
from jax import lax
from jax.experimental import pallas as pl
from jax.experimental.pallas import tpu as pltpu
from jax.sharding import PartitionSpec as P

D = 2304


epsilon = 1e-06


def gated_unit(gate, up):
    return jax.nn.gelu(gate, approximate=True) * up


def shards(tokens, hidden_grad, norm_gain, w_gate, w_up):
    n_dp = lax.axis_size("dp")
    n_model = lax.axis_size(("tp", "section"))
    rows_in = lax.all_gather(tokens, "section", axis=1, tiled=True)
    inputs = rows_in.astype(jnp.float32)
    inv_rms = lax.rsqrt(jnp.mean(inputs * inputs, axis=1) + epsilon)
    normed = (inputs * inv_rms[:, None] * norm_gain).astype(jnp.bfloat16)
    per_device, features = normed.shape
    cols_normed = lax.all_to_all(normed, "dp", split_axis=1, concat_axis=0, tiled=True)
    width = w_gate.shape[1]
    part_gate = jnp.dot(cols_normed, w_gate, preferred_element_type=jnp.float32)
    part_up = jnp.dot(cols_normed, w_up, preferred_element_type=jnp.float32)
    parts = jnp.concatenate([part_gate, part_up], axis=1).astype(jnp.bfloat16)
    parts = lax.all_to_all(parts, "dp", split_axis=0, concat_axis=0, tiled=True)
    sums = jnp.sum(parts.reshape(n_dp, per_device, 2 * width).astype(jnp.float32), axis=0)
    gate, up = sums[:, :width], sums[:, width:]
    hidden, pull = jax.vjp(gated_unit, gate, up)
    d_both = jnp.concatenate(pull(hidden_grad.astype(jnp.float32)), axis=1).astype(jnp.bfloat16)
    d_all = lax.all_gather(d_both, "dp", axis=0, tiled=True)
    d_gate, d_up = d_all[:, :width], d_all[:, width:]
    contract_cols = (((1,), (1,)), ((), ()))
    contract_rows = (((0,), (0,)), ((), ()))
    first = lax.dot_general(w_gate, d_gate, contract_cols, preferred_element_type=jnp.float32)
    second = lax.dot_general(w_up, d_up, contract_cols, preferred_element_type=jnp.float32)
    own_width = features // n_model
    per_row = n_model // n_dp
    d_part = (first + second).astype(jnp.bfloat16)
    d_part = d_part.reshape(per_row, own_width, n_dp, per_device).transpose(2, 0, 1, 3)
    d_part = d_part.reshape(n_model * own_width, per_device)
    d_columns = lax.psum_scatter(d_part, ("tp", "section"), scatter_dimension=0, tiled=True)
    moves = [
        (i * n_model + o * per_row + r, o * n_model + i * per_row + r)
        for i in range(n_dp)
        for o in range(n_dp)
        for r in range(per_row)
    ]
    d_columns = lax.ppermute(d_columns, ("dp", "tp", "section"), moves)
    d_normed = d_columns.astype(jnp.float32).T
    offset = lax.axis_index(("tp", "section")) * own_width
    own_inputs = lax.dynamic_slice_in_dim(inputs, offset, own_width, 1)
    own_gain = lax.dynamic_slice_in_dim(norm_gain, offset, own_width, 0)
    gain_part = jnp.sum(d_normed * own_inputs * inv_rms[:, None], axis=0)
    row_part = jnp.sum(own_inputs * own_gain * d_normed, axis=1)
    grad_gain = lax.psum(gain_part, "dp")
    row_sum = lax.psum(row_part, ("tp", "section"))
    grad_tokens = (
        inv_rms[:, None] * own_gain * d_normed
        - own_inputs * (inv_rms**3 * row_sum / features)[:, None]
    )
    grad_gate = lax.dot_general(cols_normed, d_gate, contract_rows, preferred_element_type=jnp.float32)
    grad_up = lax.dot_general(cols_normed, d_up, contract_rows, preferred_element_type=jnp.float32)
    return (
        grad_tokens.astype(jnp.bfloat16),
        grad_gain,
        grad_gate.astype(jnp.bfloat16),
        grad_up.astype(jnp.bfloat16),
    )


MESH = pl.DeviceIdType.MESH
SQRT_2_OVER_PI = 0.7978845608028654
CUBIC = 0.044715
CHUNKS = 3
CONTRACT_COLS = (((1,), (1,)), ((), ()))


def exchange_kernel(
    full,
    x_t,
    gain,
    back_hbm,
    wg_hbm,
    wu_hbm,
    grad_t,
    gain_out,
    xg_out,
    d_out,
    wg,
    wu,
    back,
    xg_send,
    xg,
    xn,
    slab,
    squares,
    part_send,
    part_recv,
    own_part,
    d_all,
    pieces,
    incoming,
    moved,
    move_send,
    rows,
    prods,
    gains,
    sib_in,
    halved,
    load_sem,
    tok_send,
    tok_recv,
    slab_send,
    slab_recv,
    sq_send,
    sq_recv,
    part_ssem,
    part_rsem,
    d_ssem,
    d_rsem,
    piece_ssem,
    piece_rsem,
    sib_ssem,
    sib_rsem,
    last_send,
    last_recv,
    row_ssem,
    row_rsem,
):
    i, t, s = lax.axis_index("dp"), lax.axis_index("tp"), lax.axis_index("section")
    other = 1 - i
    sec_rows, per_device = x_t.shape
    own = slab.shape[0]
    gain_own = gain.at[pl.ds(pl.multiple_of((t * 4 + s) * own, 16), own)]
    half, q = s // 2, lax.rem(s, 2)
    sibling, across = s + 1 - 2 * q, s + 2 - 4 * half
    ck = wg.shape[2]
    width = CHUNKS * ck

    def to(d, tt, ss):
        return {"dp": d, "tp": tt, "section": ss}

    def send(src, dst, ssem, rsem, target):
        return pltpu.make_async_remote_copy(
            src_ref=src, dst_ref=dst, send_sem=ssem, recv_sem=rsem, device_id=target, device_id_type=MESH
        )

    barrier = pltpu.get_barrier_semaphore()
    group = [(dt, ds) for dt in range(4) for ds in range(4) if dt + ds > 0]
    swap_tp = t + 2 - 4 * (t // 2)
    everyone = [to(i, lax.rem(t + dt, 4), lax.rem(s + ds, 4)) for dt, ds in group]
    everyone += [to(other, t, s), to(other, swap_tp, s)]
    for target in everyone:
        pl.semaphore_signal(barrier, inc=1, device_id=target, device_id_type=MESH)

    loads = []
    for k in range(CHUNKS):
        cols = pl.ds(k * ck, ck)
        loads.append(
            (
                pltpu.make_async_copy(wg_hbm.at[:, cols], wg.at[k], load_sem.at[0, k]),
                pltpu.make_async_copy(wu_hbm.at[:, cols], wu.at[k], load_sem.at[1, k]),
                pltpu.make_async_copy(back_hbm.at[:, cols], back.at[k], load_sem.at[2, k]),
            )
        )
        for load in loads[-1]:
            load.start()

    raw = x_t[...].astype(jnp.float32)
    scaled = (raw * gain[pl.ds(pl.multiple_of(s * sec_rows, 16), sec_rows)]).astype(jnp.bfloat16)
    xg_send[...] = scaled
    squares[0] = jnp.broadcast_to(jnp.sum(raw * raw, axis=0, keepdims=True), squares.shape[1:])
    my_rows = pl.ds(pl.multiple_of(q * sec_rows, 16), sec_rows)

    pl.semaphore_wait(barrier, len(everyone))

    over_dp = send(xg_send, xg.at[i, my_rows], tok_send.at[0], tok_recv.at[0], to(other, t, s))
    over_y = [
        send(xg_send, xg.at[i, my_rows], tok_send.at[1], tok_recv.at[1], to(i, t, across)),
        send(xg.at[other, my_rows], xg.at[other, my_rows], tok_send.at[2], tok_recv.at[2], to(i, t, across)),
    ]
    over_core = [
        send(xg.at[g, my_rows], xg.at[g, my_rows], tok_send.at[3 + n], tok_recv.at[3 + n], to(i, t, sibling))
        for n, g in enumerate((i, other))
    ]

    @pl.when(half != i)
    def _():
        over_dp.start()

    @pl.when(half == i)
    def _():
        over_y[0].start()
        xg[i, my_rows] = scaled

    square_sends = []
    for ds in range(1, 4):
        copy = send(
            squares.at[0], squares.at[ds], sq_send.at[ds], sq_recv.at[ds], to(i, t, lax.rem(s + ds, 4))
        )
        copy.start()
        square_sends.append(copy)

    @pl.when(half != i)
    def _():
        over_y[0].wait_recv()

    over_core[0].start()

    @pl.when(half == i)
    def _():
        over_dp.wait_recv()
        over_y[1].start()

    @pl.when(half != i)
    def _():
        over_y[1].wait_recv()

    over_core[1].start()

    def slab_copy(ds):
        ss = lax.rem(s + ds, 4)
        there = pl.ds(pl.multiple_of(ss * own, 16), own)
        return send(x_t.at[there], slab, slab_send.at[ds], slab_recv, to(i, t, ss))

    @pl.when(s == t)
    def _():
        for ds in range(1, 4):
            slab_copy(ds).start()
        slab[...] = x_t[pl.ds(pl.multiple_of(s * own, 16), own)]

    over_core[1].wait_recv()
    xn[other] = xg[other].T
    part_sends = []
    for k in range(CHUNKS):
        for load in loads[k]:
            load.wait()
        for n, w in enumerate((wg, wu)):
            part_send[k, :, pl.ds(n * ck, ck)] = jnp.dot(
                xn[other], w[k], preferred_element_type=jnp.float32
            ).astype(jnp.bfloat16)
        copy = send(part_send.at[k], part_recv.at[k], part_ssem.at[k], part_rsem.at[k], to(other, t, s))
        copy.start()
        part_sends.append(copy)

    over_core[0].wait_recv()
    xn[i] = xg[i].T
    for k in range(CHUNKS):
        for n, w in enumerate((wg, wu)):
            own_part[k, :, pl.ds(n * ck, ck)] = jnp.dot(xn[i], w[k], preferred_element_type=jnp.float32)
    for copy in square_sends:
        copy.wait()
    total = squares[0] + squares[1] + squares[2] + squares[3]
    inv_row = lax.rsqrt(total[:1] / full + epsilon)
    inv = jnp.broadcast_to(inv_row, (per_device, per_device)).T[:, :1]

    d_sends = []
    row_col = jnp.zeros((per_device, 1), jnp.float32)
    for k in range(CHUNKS):
        part_sends[k].wait_recv()
        raw_sums = own_part[k] + part_recv[k].astype(jnp.float32)
        gate, up = raw_sums[:, :ck] * inv, raw_sums[:, ck:] * inv
        grad = back[k].astype(jnp.float32) * inv
        square = gate * gate
        th = jnp.tanh(SQRT_2_OVER_PI * gate * (1.0 + CUBIC * square))
        cdf = 0.5 * (1.0 + th)
        slope = cdf + 0.5 * gate * (1.0 - th * th) * (SQRT_2_OVER_PI * (1.0 + 3.0 * CUBIC * square))
        d_gate, d_up = grad * up * slope, grad * gate * cdf
        d_all[i, k, :, pl.ds(0, ck)] = d_gate.astype(jnp.bfloat16)
        d_all[i, k, :, pl.ds(ck, ck)] = d_up.astype(jnp.bfloat16)
        copy = send(d_all.at[i, k], d_all.at[i, k], d_ssem.at[k], d_rsem.at[k], to(other, t, s))
        copy.start()
        d_sends.append(copy)
        terms = d_gate * raw_sums[:, :ck] + d_up * raw_sums[:, ck:]
        row_col = row_col + jnp.sum(terms, axis=1, keepdims=True)

    rows[0] = jnp.broadcast_to(row_col, (per_device, per_device)).T[:8]
    row_sends = []
    for dt, ds in group:
        slot = dt * 4 + ds
        copy = send(
            rows.at[0],
            rows.at[slot],
            row_ssem.at[slot],
            row_rsem.at[slot],
            to(i, lax.rem(t + dt, 4), lax.rem(s + ds, 4)),
        )
        copy.start()
        row_sends.append(copy)

    piece_sends = []
    for n, g in enumerate((i, other)):
        acc = None
        for k in range(CHUNKS):
            if n == 1:
                d_sends[k].wait_recv()
            for m, w in enumerate((wg, wu)):
                term = lax.dot_general(
                    w[k], d_all[g, k, :, pl.ds(m * ck, ck)], CONTRACT_COLS, preferred_element_type=jnp.float32
                )
                acc = term if acc is None else acc + term
        for r in range(8):
            pieces[n, r // 2, r % 2] = acc[r * own : (r + 1) * own].astype(jnp.bfloat16)
        swap = send(
            pieces.at[n, :, 1 - q], sib_in.at[n], sib_ssem.at[n], sib_rsem.at[n], to(i, t, sibling)
        )
        swap.start()
        swap.wait_recv()
        for r in range(4):
            halved[n, r] = (
                pieces[n, r, q].astype(jnp.float32) + sib_in[n, r].astype(jnp.float32)
            ).astype(jnp.bfloat16)
        piece_sends.append((swap, None, False))
        for e in (1, 0):
            tt = 2 * g + lax.rem(t + e, 2)
            dt = lax.rem(tt - t + 4, 4)
            for dy in (1, 0):
                ss = across if dy else s
                r = lax.rem(tt, 2) * 2 + ss // 2
                slot = dt * 2 + dy
                copy = send(
                    halved.at[n, r],
                    incoming.at[slot],
                    piece_ssem.at[n, e * 2 + dy],
                    piece_rsem.at[slot],
                    to(i, tt, ss),
                )
                maybe_self = e == 0 and dy == 0
                if maybe_self:

                    @pl.when(dt == 0)
                    def _(r=r, n=n):
                        incoming[0] = halved[n, r]

                    @pl.when(dt != 0)
                    def _(copy=copy):
                        copy.start()

                else:
                    copy.start()
                piece_sends.append((copy, dt, maybe_self))

    xg_out[...] = xg[...]
    d_out[...] = d_all[...]
    for copy in row_sends:
        copy.wait()

    for slot in range(1, 8):
        send(
            halved.at[0, 0], incoming.at[slot], piece_ssem.at[0, 0], piece_rsem.at[slot], to(other, t, s)
        ).wait_recv()
    d_sum = incoming[0].astype(jnp.float32)
    for slot in range(1, 8):
        d_sum = d_sum + incoming[slot].astype(jnp.float32)

    move = send(move_send, moved, last_send.at[0], last_recv.at[0], to(other, swap_tp, s))
    moved_f32 = prods.at[1, pl.ds(0, own)]
    moved_f32[...] = d_sum

    @pl.when(t // 2 != i)
    def _():
        move_send[...] = d_sum.astype(jnp.bfloat16)
        move.start()
        move.wait()
        moved_f32[...] = moved[...].astype(jnp.float32)

    @pl.when(s != t)
    def _():
        slab_copy(1).wait_recv()

    d_own = moved_f32[...]
    mine = slab[...].astype(jnp.float32)
    prods[0] = jnp.zeros(prods.shape[1:], jnp.float32)
    prods[0, pl.ds(0, own)] = mine * d_own
    gains[0] = jnp.broadcast_to(jnp.sum(prods[0].T, axis=0, keepdims=True), gains.shape[1:])
    gain_copy = send(gains.at[0], gains.at[1], last_send.at[1], last_recv.at[1], to(other, t, s))
    gain_copy.start()
    row_sum = rows[0]
    for slot in range(1, 16):
        row_sum = row_sum + rows[slot]
    factor = inv_row * inv_row * row_sum[:1] / full
    grad_t[...] = (gain_own[...] * d_own - mine * factor).astype(jnp.bfloat16)
    gain_copy.wait()
    gain_out[...] = gains[0] + gains[1]

    @pl.when(half != i)
    def _():
        over_dp.wait_send()

    @pl.when(half == i)
    def _():
        over_y[0].wait_send()
        over_y[1].wait_send()

    @pl.when(s == t)
    def _():
        for ds in range(1, 4):
            slab_copy(ds).wait_send()

    for copy in over_core + part_sends + d_sends:
        copy.wait_send()
    for copy, dt, maybe_self in piece_sends:
        if maybe_self:

            @pl.when(dt != 0)
            def _(copy=copy):
                copy.wait_send()

        else:
            copy.wait_send()


def weight_grad_kernel(xg, d, grad_gate, grad_up):
    features = jnp.concatenate([xg[0], xg[1]], axis=1)
    rows = jnp.concatenate([d[0, 0], d[1, 0]], axis=0)
    ck = grad_gate.shape[1]
    grad_gate[...] = jnp.dot(features, rows[:, :ck], preferred_element_type=jnp.float32).astype(jnp.bfloat16)
    grad_up[...] = jnp.dot(features, rows[:, ck:], preferred_element_type=jnp.float32).astype(jnp.bfloat16)


def fused_shards(tokens, hidden_grad, norm_gain, w_gate, w_up):
    per_device, sec_rows = tokens.shape
    block, width = w_gate.shape
    full = norm_gain.shape[0]
    own = full // 16
    ck = width // CHUNKS
    bf, f32 = jnp.bfloat16, jnp.float32
    vmem = pl.BlockSpec(memory_space=pltpu.VMEM)
    anywhere = pl.BlockSpec(memory_space=pltpu.HBM)
    dma = pltpu.SemaphoreType.DMA
    own_pad = pl.cdiv(own, 128) * 128
    grad_t, gain_sum, xg, d_all = pl.pallas_call(
        functools.partial(exchange_kernel, full),
        out_shape=(
            jax.ShapeDtypeStruct((own, per_device), bf),
            jax.ShapeDtypeStruct((8, own_pad), f32),
            jax.ShapeDtypeStruct((2, block, per_device), bf),
            jax.ShapeDtypeStruct((2, CHUNKS, per_device, 2 * ck), bf),
        ),
        in_specs=[vmem, vmem, anywhere, anywhere, anywhere],
        out_specs=(vmem, vmem, vmem, vmem),
        scratch_shapes=[
            pltpu.VMEM((CHUNKS, block, ck), bf),
            pltpu.VMEM((CHUNKS, block, ck), bf),
            pltpu.VMEM((CHUNKS, per_device, ck), bf),
            pltpu.VMEM((sec_rows, per_device), bf),
            pltpu.VMEM((2, block, per_device), bf),
            pltpu.VMEM((2, per_device, block), bf),
            pltpu.VMEM((own, per_device), bf),
            pltpu.VMEM((4, 8, per_device), f32),
            pltpu.VMEM((CHUNKS, per_device, 2 * ck), bf),
            pltpu.VMEM((CHUNKS, per_device, 2 * ck), bf),
            pltpu.VMEM((CHUNKS, per_device, 2 * ck), f32),
            pltpu.VMEM((2, CHUNKS, per_device, 2 * ck), bf),
            pltpu.VMEM((2, 4, 2, own, per_device), bf),
            pltpu.VMEM((8, own, per_device), bf),
            pltpu.VMEM((own, per_device), bf),
            pltpu.VMEM((own, per_device), bf),
            pltpu.VMEM((16, 8, per_device), f32),
            pltpu.VMEM((2, own_pad, per_device), f32),
            pltpu.VMEM((2, 8, own_pad), f32),
            pltpu.VMEM((2, 4, own, per_device), bf),
            pltpu.VMEM((2, 4, own, per_device), bf),
            dma((3, CHUNKS)),
            dma((5,)),
            dma((5,)),
            dma((4,)),
            dma,
            dma((4,)),
            dma((4,)),
            dma((CHUNKS,)),
            dma((CHUNKS,)),
            dma((CHUNKS,)),
            dma((CHUNKS,)),
            dma((2, 4)),
            dma((8,)),
            dma((2,)),
            dma((2,)),
            dma((2,)),
            dma((2,)),
            dma((16,)),
            dma((16,)),
        ],
        compiler_params=pltpu.CompilerParams(
            collective_id=0, has_side_effects=True, vmem_limit_bytes=51 * 1024 * 1024
        ),
    )(tokens.T, norm_gain[:, None], hidden_grad, w_gate, w_up)
    grad_gate, grad_up = pl.pallas_call(
        weight_grad_kernel,
        grid=(CHUNKS,),
        out_shape=(jax.ShapeDtypeStruct((block, width), bf),) * 2,
        in_specs=[
            pl.BlockSpec((2, block, per_device), lambda k: (0, 0, 0)),
            pl.BlockSpec((2, 1, per_device, 2 * ck), lambda k: (0, k, 0, 0)),
        ],
        out_specs=(pl.BlockSpec((block, ck), lambda k: (0, k)),) * 2,
        compiler_params=pltpu.CompilerParams(vmem_limit_bytes=40 * 1024 * 1024),
    )(xg, d_all)
    return grad_t.T, gain_sum[0, :own], grad_gate, grad_up


def solution(mesh):
    in_specs = (
        P("dp", "section"),
        P("dp", ("tp", "section")),
        P(),
        P("dp", ("tp", "section")),
        P("dp", ("tp", "section")),
    )
    out_specs = (
        P("dp", ("tp", "section")),
        P(("tp", "section")),
        P("dp", ("tp", "section")),
        P("dp", ("tp", "section")),
    )
    sizes = tuple(mesh.shape[a] for a in ("dp", "tp", "section"))
    body = fused_shards if sizes == (2, 4, 4) else shards
    return jax.shard_map(body, mesh=mesh, in_specs=in_specs, out_specs=out_specs, check_vma=False)
```

profile of v0, /device:TPU:0, one launch (start us, length us, event | category | flops | bytes accessed | tf_op | source)
XLA Modules:
  0.0 70.4 jit_solution(14606564086850190582)
XLA Ops:
  0.6 2.1 %broadcast_in_dim.4.gain = f32[2304,1]{1,0:T(8,128)} reshape(f32[2304]{0:T(1024)} %param.7) | data formatting | bytes 18432 | tf_op jit(solution)/shard_map/broadcast_in_dim | solution.py:495
  2.7 0.0 copy-start
  2.7 1.0 %copy-done = bf16[128,1152]{1,0:T(8,128)(2,1)S(1)} copy-done((bf16[128,1152]{1,0:T(8,128)(2,1)S(1)}, bf16[128,1152]{1,0:T(8,128)(2,1)}, u32[]{:S(2)}) %copy-start) | copy-done | bytes 294936
  3.7 0.0 copy-start.1
  3.7 0.9 %copy-done.1 = bf16[128,576]{0,1:T(8,128)(2,1)S(1)} copy-done((bf16[128,576]{0,1:T(8,128)(2,1)S(1)}, bf16[128,576]{0,1:T(8,128)(2,1)}, u32[]{:S(2)}) %copy-start.1) | copy-done | bytes 147480
  4.6 61.1 %shard_map.84 = (bf16[144,128]{1,0:T(8,128)(2,1)S(1)}, f32[8,256]{1,0:T(8,128)S(1)}, bf16[2,1152,128]{2,1,0:T(8,128)(2,1)S(1)}, bf16[2,3,128,768]{3,2,1,0:T(8,128)(2,1)S(1)}) custom-call(bf16[576,128]{1,0:T(8,128)(2,1)S(1)} %bitcast.3, f32[2304,1]{1,0:T(8,128)} %broadcast_in_dim.4.gain, bf16[128,1152]{1,0:T(8,128)(2,1)S(1)} %copy-done, ...), custom_call_target="tpu_custom_call" | custom-call | tf_op jit(solution)/shard_map/pallas_call | solution.py:440
  65.7 0.6 slice.3
  66.3 3.5 %shard_map.85 = (bf16[1152,1152]{1,0:T(8,128)(2,1)}, bf16[1152,1152]{1,0:T(8,128)(2,1)}) custom-call(bf16[2,1152,128]{2,1,0:T(8,128)(2,1)S(1)} %get-tuple-element.12.xg, bf16[2,3,128,768]{3,2,1,0:T(8,128)(2,1)S(1)} %get-tuple-element.13.d), custom_call_target="tpu_custom_call" | custom-call | tf_op jit(solution)/shard_map/pallas_call | solution.py:496
  69.7 0.6 copy.11
Async XLA Ops:
  2.7 1.0 %copy-start = (bf16[128,1152]{1,0:T(8,128)(2,1)S(1)}, bf16[128,1152]{1,0:T(8,128)(2,1)}, u32[]{:S(2)}) copy-start(bf16[128,1152]{1,0:T(8,128)(2,1)} %back_hbm.1) | copy-start | bytes 884740
  3.7 0.9 %copy-start.1 = (bf16[128,576]{0,1:T(8,128)(2,1)S(1)}, bf16[128,576]{0,1:T(8,128)(2,1)}, u32[]{:S(2)}) copy-start(bf16[128,576]{0,1:T(8,128)(2,1)} %param.5) | copy-start | bytes 442372
where the time goes:
time: 70.6 us; the launch traced here: 70.4 us
  Pallas kernels  64.6 us (92%)
  local copies, waits for them, and re-layouts  5.14 us (7%)
    pallas_call x1, Pallas kernels, fused_shards(): pl.pallas_call(functools.partial(exchange_kernel, full), out_shape=(jax.S...  61.1 us
    pallas_call x1, Pallas kernels, fused_shards(): pl.pallas_call(weight_grad_kernel, grid=(CHUNKS,), out_shape=(jax.ShapeDt...  3.46 us
    unnamed x5, local copies, waits for them, and re-layouts  2.49 us
    broadcast_in_dim x1, local copies, waits for them, and re-layouts, fused_shards(): norm_gain[:, None]  2.09 us

commit v1 on v0

v1 whole, which is shorter than its diff:
```python
import functools

import jax
import jax.numpy as jnp
from jax import lax
from jax.experimental import pallas as pl
from jax.experimental.pallas import tpu as pltpu
from jax.sharding import PartitionSpec as P

D = 2304


epsilon = 1e-06


def gated_unit(gate, up):
    return jax.nn.gelu(gate, approximate=True) * up


def shards(tokens, hidden_grad, norm_gain, w_gate, w_up):
    n_dp = lax.axis_size("dp")
    n_model = lax.axis_size(("tp", "section"))
    rows_in = lax.all_gather(tokens, "section", axis=1, tiled=True)
    inputs = rows_in.astype(jnp.float32)
    inv_rms = lax.rsqrt(jnp.mean(inputs * inputs, axis=1) + epsilon)
    normed = (inputs * inv_rms[:, None] * norm_gain).astype(jnp.bfloat16)
    per_device, features = normed.shape
    cols_normed = lax.all_to_all(normed, "dp", split_axis=1, concat_axis=0, tiled=True)
    width = w_gate.shape[1]
    part_gate = jnp.dot(cols_normed, w_gate, preferred_element_type=jnp.float32)
    part_up = jnp.dot(cols_normed, w_up, preferred_element_type=jnp.float32)
    parts = jnp.concatenate([part_gate, part_up], axis=1).astype(jnp.bfloat16)
    parts = lax.all_to_all(parts, "dp", split_axis=0, concat_axis=0, tiled=True)
    sums = jnp.sum(parts.reshape(n_dp, per_device, 2 * width).astype(jnp.float32), axis=0)
    gate, up = sums[:, :width], sums[:, width:]
    hidden, pull = jax.vjp(gated_unit, gate, up)
    d_both = jnp.concatenate(pull(hidden_grad.astype(jnp.float32)), axis=1).astype(jnp.bfloat16)
    d_all = lax.all_gather(d_both, "dp", axis=0, tiled=True)
    d_gate, d_up = d_all[:, :width], d_all[:, width:]
    contract_cols = (((1,), (1,)), ((), ()))
    contract_rows = (((0,), (0,)), ((), ()))
    first = lax.dot_general(w_gate, d_gate, contract_cols, preferred_element_type=jnp.float32)
    second = lax.dot_general(w_up, d_up, contract_cols, preferred_element_type=jnp.float32)
    own_width = features // n_model
    per_row = n_model // n_dp
    d_part = (first + second).astype(jnp.bfloat16)
    d_part = d_part.reshape(per_row, own_width, n_dp, per_device).transpose(2, 0, 1, 3)
    d_part = d_part.reshape(n_model * own_width, per_device)
    d_columns = lax.psum_scatter(d_part, ("tp", "section"), scatter_dimension=0, tiled=True)
    moves = [
        (i * n_model + o * per_row + r, o * n_model + i * per_row + r)
        for i in range(n_dp)
        for o in range(n_dp)
        for r in range(per_row)
    ]
    d_columns = lax.ppermute(d_columns, ("dp", "tp", "section"), moves)
    d_normed = d_columns.astype(jnp.float32).T
    offset = lax.axis_index(("tp", "section")) * own_width
    own_inputs = lax.dynamic_slice_in_dim(inputs, offset, own_width, 1)
    own_gain = lax.dynamic_slice_in_dim(norm_gain, offset, own_width, 0)
    gain_part = jnp.sum(d_normed * own_inputs * inv_rms[:, None], axis=0)
    row_part = jnp.sum(own_inputs * own_gain * d_normed, axis=1)
    grad_gain = lax.psum(gain_part, "dp")
    row_sum = lax.psum(row_part, ("tp", "section"))
    grad_tokens = (
        inv_rms[:, None] * own_gain * d_normed
        - own_inputs * (inv_rms**3 * row_sum / features)[:, None]
    )
    grad_gate = lax.dot_general(cols_normed, d_gate, contract_rows, preferred_element_type=jnp.float32)
    grad_up = lax.dot_general(cols_normed, d_up, contract_rows, preferred_element_type=jnp.float32)
    return (
        grad_tokens.astype(jnp.bfloat16),
        grad_gain,
        grad_gate.astype(jnp.bfloat16),
        grad_up.astype(jnp.bfloat16),
    )


MESH = pl.DeviceIdType.MESH
SQRT_2_OVER_PI = 0.7978845608028654
CUBIC = 0.044715
CHUNKS = 3
HALVES = 2
CONTRACT_COLS = (((1,), (1,)), ((), ()))


def exchange_kernel(
    full,
    x_hbm,
    gain_hbm,
    back_hbm,
    wg_hbm,
    wu_hbm,
    grad_t,
    gain_out,
    grad_gate,
    grad_up,
    x_in,
    gain_in,
    gain_col,
    w,
    back,
    relay,
    xg,
    xs,
    xn,
    slab,
    squares,
    part_send,
    part_recv,
    own_part,
    d_all,
    own_pieces,
    own_sib,
    own_halved,
    own_incoming,
    pieces,
    sib_in,
    halved,
    incoming,
    move_send,
    moved,
    rows,
    prods,
    gains,
    load_sem,
    w_sem,
    tok_send,
    tok_recv,
    core_send,
    core_recv,
    slab_send,
    slab_recv,
    sq_send,
    sq_recv,
    part_ssem,
    part_rsem,
    d_ssem,
    d_rsem,
    own_ssem,
    own_rsem,
    piece_ssem,
    piece_rsem,
    sib_ssem,
    sib_rsem,
    last_send,
    last_recv,
    row_ssem,
    row_rsem,
):
    i, t, s = lax.axis_index("dp"), lax.axis_index("tp"), lax.axis_index("section")
    other = 1 - i
    f32, bf = jnp.float32, jnp.bfloat16
    sec_rows, per_device = x_in.shape
    own = slab.shape[0]
    block = 2 * sec_rows
    half, q = s // 2, lax.rem(s, 2)
    sibling, across = s + 1 - 2 * q, s + 2 - 4 * half
    ck = back.shape[2]
    th = per_device // HALVES
    fold = own // 2
    cut = sec_rows // 2
    reducer = t // 2 == i

    def to(d, tt, ss):
        return {"dp": d, "tp": tt, "section": ss}

    def send(src, dst, ssem, rsem, target):
        return pltpu.make_async_remote_copy(
            src_ref=src, dst_ref=dst, send_sem=ssem, recv_sem=rsem, device_id=target, device_id_type=MESH
        )

    barrier = pltpu.get_barrier_semaphore()
    group = [(dt, ds) for dt in range(4) for ds in range(4) if dt + ds > 0]
    everyone = [to(i, lax.rem(t + dt, 4), lax.rem(s + ds, 4)) for dt, ds in group]
    everyone += [to(other, t, s)]
    for target in everyone:
        pl.semaphore_signal(barrier, inc=1, device_id=target, device_id_type=MESH)

    x_load = pltpu.make_async_copy(x_hbm, x_in, load_sem.at[0])
    gain_load = pltpu.make_async_copy(gain_hbm, gain_in, load_sem.at[1])
    x_load.start()
    gain_load.start()
    loads = []
    for k in range(CHUNKS):
        cols = pl.ds(k * ck, ck)
        loads.append(
            (
                pltpu.make_async_copy(wg_hbm.at[:, cols], w.at[k, :, pl.ds(0, ck)], w_sem.at[0, k]),
                pltpu.make_async_copy(wu_hbm.at[:, cols], w.at[k, :, pl.ds(ck, ck)], w_sem.at[1, k]),
                pltpu.make_async_copy(back_hbm.at[:, cols], back.at[k], w_sem.at[2, k]),
            )
        )
        for load in loads[-1]:
            load.start()

    def seg(part):
        return pl.ds(pl.multiple_of(q * sec_rows + part * cut, 16), cut)

    my_rows = pl.ds(pl.multiple_of(q * sec_rows, 16), sec_rows)
    first, second = pl.ds(0, cut), pl.ds(cut, cut)
    xdev, ydev, cdev = to(other, t, s), to(i, t, across), to(i, t, sibling)

    def token_copy(n, m, src, dst, target):
        return send(src, dst, tok_send.at[n], tok_recv.at[m], target)

    x_first = token_copy(0, 0, x_in.at[first], xg.at[1, seg(0)], xdev)
    x_second = token_copy(1, 1, x_in.at[second], xg.at[1, seg(1)], xdev)
    y_second = token_copy(2, 3, x_in.at[second], relay, ydev)
    y_own = token_copy(0, 2, x_in, xg.at[0, my_rows], ydev)
    y_first = token_copy(1, 0, xg.at[1, seg(0)], xg.at[1, seg(0)], ydev)
    x_relay = token_copy(2, 1, relay, xg.at[1, seg(1)], xdev)
    core_own_in = send(x_in, xg.at[0, my_rows], core_send.at[2], core_recv.at[2], cdev)
    core_own = send(xg.at[0, my_rows], xg.at[0, my_rows], core_send.at[2], core_recv.at[2], cdev)
    core_other = [
        send(xg.at[1, seg(p)], xg.at[1, seg(p)], core_send.at[p], core_recv.at[p], cdev) for p in range(2)
    ]

    x_load.wait()
    raw = x_in[...].astype(f32)
    squares[0] = jnp.broadcast_to(jnp.sum(raw * raw, axis=0, keepdims=True), squares.shape[1:])

    pl.semaphore_wait(barrier, len(everyone))

    @pl.when(half != i)
    def _():
        x_first.start()
        y_second.start()
        x_second.start()

    @pl.when(half == i)
    def _():
        y_own.start()
        core_own_in.start()
        xg[0, my_rows] = x_in[...]

    square_sends = []
    for ds in range(1, 4):
        copy = send(
            squares.at[0], squares.at[ds], sq_send.at[ds], sq_recv.at[ds], to(i, t, lax.rem(s + ds, 4))
        )
        copy.start()
        square_sends.append(copy)

    def slab_copy(ds):
        ss = lax.rem(s + ds, 4)
        there = pl.ds(pl.multiple_of(ss * own, 16), own)
        return send(x_in.at[there], slab, slab_send.at[ds], slab_recv, to(i, t, ss))

    @pl.when(s == t)
    def _():
        for ds in range(1, 4):
            slab_copy(ds).start()
        slab[...] = x_in[pl.ds(pl.multiple_of(s * own, 16), own)]

    gain_load.wait()
    n_rows = gain_in.shape[0]
    filled = jnp.concatenate([gain_in[...], jnp.zeros((128 - n_rows, 128), f32)], axis=0).T
    for b in range(n_rows):
        gain_col[b * 128 : (b + 1) * 128] = jnp.broadcast_to(filled[:, b : b + 1], (128, 128))

    @pl.when(half == i)
    def _():
        x_first.wait_recv()
        y_first.start()

    @pl.when(half != i)
    def _():
        y_own.wait_recv()
        core_own.start()
        y_first.wait_recv()

    core_other[0].start()

    @pl.when(half == i)
    def _():
        y_second.wait_recv()
        x_relay.start()

    x_second.wait_recv()
    core_other[1].start()

    half_gain = gain_col.at[pl.ds(pl.multiple_of(i * block, 16), block)]

    def scale(slot):
        scaled = (xg[slot].astype(f32) * half_gain[...]).astype(bf)
        xs[:, slot * per_device : (slot + 1) * per_device] = scaled
        xn[slot] = scaled.T

    core_other[0].wait_recv()
    core_other[1].wait_recv()
    scale(1)
    part_sends = {}
    for h in range(HALVES):
        for k in range(CHUNKS):
            if h == 0:
                for load in loads[k]:
                    load.wait()
            part_send[h, k] = jnp.dot(
                xn[1, h * th : (h + 1) * th], w[k], preferred_element_type=f32
            ).astype(bf)
            copy = send(part_send.at[h, k], part_recv.at[h, k], part_ssem.at[h, k], part_rsem.at[h, k], xdev)
            copy.start()
            part_sends[h, k] = copy

    core_own.wait_recv()
    scale(0)
    for k in range(CHUNKS):
        own_part[k] = jnp.dot(xn[0], w[k], preferred_element_type=f32)
    for copy in square_sends:
        copy.wait()
    total = squares[0] + squares[1] + squares[2] + squares[3]
    inv_row = lax.rsqrt(total[:1] / full + epsilon)
    inv_all = jnp.broadcast_to(inv_row, (per_device, per_device)).T[:, :1]

    d_sends = {}
    row_cols = []
    for h in range(HALVES):
        here = slice(h * th, (h + 1) * th)
        inv = inv_all[here]
        row_col = jnp.zeros((th, 1), f32)
        for k in range(CHUNKS):
            part_sends[h, k].wait_recv()
            raw_sums = own_part[k, here] + part_recv[h, k].astype(f32)
            gate, up = raw_sums[:, :ck] * inv, raw_sums[:, ck:] * inv
            grad = back[k, here].astype(f32) * inv
            square = gate * gate
            tanh = jnp.tanh(SQRT_2_OVER_PI * gate * (1.0 + CUBIC * square))
            cdf = 0.5 * (1.0 + tanh)
            slope = cdf + 0.5 * gate * (1.0 - tanh * tanh) * (SQRT_2_OVER_PI * (1.0 + 3.0 * CUBIC * square))
            d_gate, d_up = grad * up * slope, grad * gate * cdf
            d_all[0, k, here, pl.ds(0, ck)] = d_gate.astype(bf)
            d_all[0, k, here, pl.ds(ck, ck)] = d_up.astype(bf)
            tokens_here = pl.ds(h * th, th)
            copy = send(
                d_all.at[0, k, tokens_here], d_all.at[1, k, tokens_here], d_ssem.at[h, k], d_rsem.at[h, k], xdev
            )
            copy.start()
            d_sends[h, k] = copy
            terms = d_gate * raw_sums[:, :ck] + d_up * raw_sums[:, ck:]
            row_col = row_col + jnp.sum(terms, axis=1, keepdims=True)
        row_cols.append(row_col)

    row_col = jnp.concatenate(row_cols, axis=0)
    rows[0] = jnp.broadcast_to(row_col, (per_device, per_device)).T[:8]
    row_sends = []
    for dt, ds in group:
        slot = dt * 4 + ds
        copy = send(
            rows.at[0],
            rows.at[slot],
            row_ssem.at[slot],
            row_rsem.at[slot],
            to(i, lax.rem(t + dt, 4), lax.rem(s + ds, 4)),
        )
        copy.start()
        row_sends.append(copy)

    def scatter(parts, landing, ssem, rsem):
        copies = []
        for e in (1, 0):
            tt = 2 * i + lax.rem(t + e, 2)
            dt = lax.rem(tt - t + 4, 4)
            for dy in (1, 0):
                ss = across if dy else s
                r = lax.rem(tt, 2) * 2 + ss // 2
                slot = dt * 2 + dy
                copy = send(parts.at[r], landing.at[slot], ssem.at[e * 2 + dy], rsem.at[slot], to(i, tt, ss))
                maybe_self = e == 0 and dy == 0
                if maybe_self:

                    @pl.when(dt == 0)
                    def _(r=r):
                        landing[0] = parts[r]

                    @pl.when(dt != 0)
                    def _(copy=copy):
                        copy.start()

                else:
                    copy.start()
                copies.append((copy, dt, maybe_self))
        return copies

    def gathered(parts, landing, ssem, rsem):
        for slot in range(1, 8):
            send(parts.at[0], landing.at[slot], ssem.at[0], rsem.at[slot], xdev).wait_recv()
        result = landing[0].astype(f32)
        for slot in range(1, 8):
            result = result + landing[slot].astype(f32)
        return result

    acc = None
    for k in range(CHUNKS):
        term = lax.dot_general(w[k], d_all[0, k], CONTRACT_COLS, preferred_element_type=f32)
        acc = term if acc is None else acc + term
    for r in range(8):
        own_pieces[r % 2, r // 2] = acc[r * own : (r + 1) * own].astype(bf)
    own_swap = send(own_pieces.at[1 - q], own_sib, sib_ssem.at[HALVES], sib_rsem.at[HALVES], cdev)
    own_swap.start()
    own_swap.wait_recv()
    own_halved[...] = (own_pieces[q].astype(f32) + own_sib[...].astype(f32)).astype(bf)
    piece_sends = scatter(own_halved, own_incoming, own_ssem, own_rsem)

    def weight_grads(k):
        both = jnp.concatenate([d_all[0, k], d_all[1, k]], axis=0)
        cols = pl.ds(k * ck, ck)
        grad_gate[:, cols] = jnp.dot(xs[...], both[:, :ck], preferred_element_type=f32).astype(bf)
        grad_up[:, cols] = jnp.dot(xs[...], both[:, ck:], preferred_element_type=f32).astype(bf)

    lane = lax.broadcasted_iota(jnp.int32, (fold, per_device), 1)
    left = lane < th
    swaps = []
    for h in range(HALVES):
        acc = None
        for k in range(CHUNKS):
            d_sends[h, k].wait_recv()
            late = d_all[1, k, h * th : (h + 1) * th]
            twice = jnp.concatenate([late, late], axis=0)
            term = lax.dot_general(w[k], twice, CONTRACT_COLS, preferred_element_type=f32)
            acc = term if acc is None else acc + term
            if h == HALVES - 1 and k < CHUNKS - 1:
                weight_grads(k)
        for r in range(8):
            upper, lower = acc[r * own : r * own + fold], acc[r * own + fold : (r + 1) * own]
            pieces[h, r % 2, r // 2] = jnp.where(left, upper, lower).astype(bf)
        swap = send(pieces.at[h, 1 - q], sib_in.at[h], sib_ssem.at[h], sib_rsem.at[h], cdev)
        swap.start()
        swap.wait_recv()
        swaps.append(swap)
        halved[h] = (pieces[h, q].astype(f32) + sib_in[h].astype(f32)).astype(bf)
        piece_sends += scatter(halved.at[h], incoming.at[h], piece_ssem.at[h], piece_rsem.at[h])

    weight_grads(CHUNKS - 1)
    for copy in row_sends:
        copy.wait()
    row_sum = rows[0]
    for slot in range(1, 16):
        row_sum = row_sum + rows[slot]
    factor = inv_row * inv_row * row_sum[:1] / full

    @pl.when(s != t)
    def _():
        slab_copy(1).wait_recv()

    mine = slab[...].astype(f32)
    gain_own = gain_col[pl.ds(pl.multiple_of((t * 4 + s) * own, 16), own)]

    def moves(h):
        return send(move_send.at[h], moved.at[h], last_send.at[h], last_recv.at[h], xdev)

    gain_copy = send(gains.at[0], gains.at[1], last_send.at[HALVES], last_recv.at[HALVES], xdev)

    @pl.when(reducer)
    def _():
        d_own = gathered(own_halved, own_incoming, own_ssem, own_rsem)
        grad_t[...] = (gain_own * d_own - mine * factor).astype(bf)
        prods[pl.ds(0, own)] = mine * d_own
        prods[pl.ds(own, prods.shape[0] - own)] = jnp.zeros((prods.shape[0] - own, per_device), f32)
        local = pl.multiple_of((lax.rem(t, 2) * 4 + s) * own, 16)
        theirs = xg[1, pl.ds(local, own)].astype(f32)
        upper, lower = theirs[:fold], theirs[fold:]
        for h in range(HALVES):
            d_late = gathered(halved.at[h], incoming.at[h], piece_ssem.at[h], piece_rsem.at[h])
            move_send[h] = d_late.astype(bf)
            moves(h).start()
            if h == 0:
                folded = jnp.where(left, upper, pltpu.roll(lower, th, 1))
            else:
                folded = jnp.where(left, pltpu.roll(upper, th, 1), lower)
            product = d_late * folded
            prods[pl.ds(0, fold)] += jnp.where(left, product, 0.0)
            prods[pl.ds(fold, fold)] += jnp.where(left, 0.0, product)
        gains[0] = jnp.broadcast_to(jnp.sum(prods[...].T, axis=0, keepdims=True), gains.shape[1:])
        gain_copy.start()
        gain_out[...] = gains[0, :1, :own]
        for h in range(HALVES):
            moves(h).wait_send()
        gain_copy.wait_send()

    @pl.when(jnp.logical_not(reducer))
    def _():
        moves(0).wait_recv()
        moves(1).wait_recv()
        early, late = moved[0].astype(f32), moved[1].astype(f32)
        upper = jnp.where(left, early, pltpu.roll(late, th, 1))
        lower = jnp.where(left, pltpu.roll(early, th, 1), late)
        grad_t[pl.ds(0, own)] = (
            gain_own * jnp.concatenate([upper, lower], axis=0) - mine * factor
        ).astype(bf)
        gain_copy.wait_recv()
        gain_out[...] = gains[1, :1, :own]

    @pl.when(half != i)
    def _():
        x_first.wait_send()
        y_second.wait_send()
        x_second.wait_send()
        core_own.wait_send()

    @pl.when(half == i)
    def _():
        y_own.wait_send()
        y_first.wait_send()
        x_relay.wait_send()
        core_own_in.wait_send()

    @pl.when(s == t)
    def _():
        for ds in range(1, 4):
            slab_copy(ds).wait_send()

    for copy in core_other + [own_swap] + swaps + list(part_sends.values()) + list(d_sends.values()):
        copy.wait_send()
    for copy, dt, maybe_self in piece_sends:
        if maybe_self:

            @pl.when(dt != 0)
            def _(copy=copy):
                copy.wait_send()

        else:
            copy.wait_send()


def write_kernel(grad_t, gain, grad_gate, grad_up, grad_t_out, gain_out, gate_out, up_out, sems):
    pairs = ((grad_gate, gate_out), (grad_up, up_out), (grad_t, grad_t_out), (gain, gain_out))
    copies = [pltpu.make_async_copy(src, dst, sems.at[n]) for n, (src, dst) in enumerate(pairs)]
    for copy in copies:
        copy.start()
    for copy in copies:
        copy.wait()


def fused_shards(tokens, hidden_grad, norm_gain, w_gate, w_up):
    per_device, sec_rows = tokens.shape
    block, width = w_gate.shape
    full = norm_gain.shape[0]
    own = full // 16
    ck = width // CHUNKS
    th = per_device // HALVES
    fold = own // 2
    bf, f32 = jnp.bfloat16, jnp.float32
    vmem = pl.BlockSpec(memory_space=pltpu.VMEM)
    anywhere = pl.BlockSpec(memory_space=pltpu.HBM)
    dma = pltpu.SemaphoreType.DMA
    own_pad = pl.cdiv(own, 128) * 128
    kept = (
        jax.ShapeDtypeStruct((own, per_device), bf),
        jax.ShapeDtypeStruct((1, own), f32),
        jax.ShapeDtypeStruct((block, width), bf),
        jax.ShapeDtypeStruct((block, width), bf),
    )
    operands = (tokens.T, norm_gain.reshape(full // 128, 128), hidden_grad, w_gate, w_up)
    results = pl.pallas_call(
        functools.partial(exchange_kernel, full),
        out_shape=tuple(pltpu.VMEM(a.shape, a.dtype) for a in kept),
        in_specs=[anywhere] * 5,
        out_specs=(vmem,) * 4,
        scratch_shapes=[
            pltpu.VMEM((sec_rows, per_device), bf),
            pltpu.VMEM((full // 128, 128), f32),
            pltpu.VMEM((full, 128), f32),
            pltpu.VMEM((CHUNKS, block, 2 * ck), bf),
            pltpu.VMEM((CHUNKS, per_device, ck), bf),
            pltpu.VMEM((sec_rows // 2, per_device), bf),
            pltpu.VMEM((2, block, per_device), bf),
            pltpu.VMEM((block, 2 * per_device), bf),
            pltpu.VMEM((2, per_device, block), bf),
            pltpu.VMEM((own, per_device), bf),
            pltpu.VMEM((4, 8, per_device), f32),
            pltpu.VMEM((HALVES, CHUNKS, th, 2 * ck), bf),
            pltpu.VMEM((HALVES, CHUNKS, th, 2 * ck), bf),
            pltpu.VMEM((CHUNKS, per_device, 2 * ck), f32),
            pltpu.VMEM((2, CHUNKS, per_device, 2 * ck), bf),
            pltpu.VMEM((2, 4, own, per_device), bf),
            pltpu.VMEM((4, own, per_device), bf),
            pltpu.VMEM((4, own, per_device), bf),
            pltpu.VMEM((8, own, per_device), bf),
            pltpu.VMEM((HALVES, 2, 4, fold, per_device), bf),
            pltpu.VMEM((HALVES, 4, fold, per_device), bf),
            pltpu.VMEM((HALVES, 4, fold, per_device), bf),
            pltpu.VMEM((HALVES, 8, fold, per_device), bf),
            pltpu.VMEM((HALVES, fold, per_device), bf),
            pltpu.VMEM((HALVES, fold, per_device), bf),
            pltpu.VMEM((16, 8, per_device), f32),
            pltpu.VMEM((own_pad, per_device), f32),
            pltpu.VMEM((2, 8, own_pad), f32),
            dma((2,)),
            dma((3, CHUNKS)),
            dma((3,)),
            dma((4,)),
            dma((3,)),
            dma((3,)),
            dma((4,)),
            dma,
            dma((4,)),
            dma((4,)),
            dma((HALVES, CHUNKS)),
            dma((HALVES, CHUNKS)),
            dma((HALVES, CHUNKS)),
            dma((HALVES, CHUNKS)),
            dma((4,)),
            dma((8,)),
            dma((HALVES, 4)),
            dma((HALVES, 8)),
            dma((HALVES + 1,)),
            dma((HALVES + 1,)),
            dma((HALVES + 1,)),
            dma((HALVES + 1,)),
            dma((16,)),
            dma((16,)),
        ],
        compiler_params=pltpu.CompilerParams(
            collective_id=0, has_side_effects=True, vmem_limit_bytes=KERNEL_MIB * 1024 * 1024
        ),
    )(*(pltpu.with_memory_space_constraint(a, pltpu.HBM) for a in operands))
    grad_t, gain, grad_gate, grad_up = pl.pallas_call(
        write_kernel,
        out_shape=kept,
        in_specs=[vmem] * 4,
        out_specs=(anywhere,) * 4,
        scratch_shapes=[dma((4,))],
        compiler_params=pltpu.CompilerParams(vmem_limit_bytes=16 * 1024 * 1024),
    )(*results)
    return grad_t.T, gain.reshape(own), grad_gate, grad_up


KERNEL_MIB = 40


def solution(mesh):
    in_specs = (
        P("dp", "section"),
        P("dp", ("tp", "section")),
        P(),
        P("dp", ("tp", "section")),
        P("dp", ("tp", "section")),
    )
    out_specs = (
        P("dp", ("tp", "section")),
        P(("tp", "section")),
        P("dp", ("tp", "section")),
        P("dp", ("tp", "section")),
    )
    sizes = tuple(mesh.shape[a] for a in ("dp", "tp", "section"))
    body = fused_shards if sizes == (2, 4, 4) else shards
    return jax.shard_map(body, mesh=mesh, in_specs=in_specs, out_specs=out_specs, check_vma=False)
```

time: 70.6 us -> 55.9 us (0.79)
  Pallas kernels: 64.6 us -> 55.1 us
  local copies, waits for them, and re-layouts: 5.14 us -> 0 us
    pallas_call x2, Pallas kernels: 64.6 us -> 55.1 us  [the longest x1 52.7 us: fused_shards(): pl.pallas_call(functools.partial(exchange_kernel, full), out_shape=tuple(...]
    unnamed x5 -> x0, local copies, waits for them, and re-layouts: 2.49 us -> none
    broadcast_in_dim x1 -> x0, local copies, waits for them, and re-layouts: 2.09 us -> none  [fused_shards(): norm_gain[:, None]]
where the time goes in v1:
time: 55.9 us; the launch traced here: 55.8 us
  Pallas kernels  55.1 us (99%)
  between operations  0.64 us (1%)
    pallas_call x1, Pallas kernels, fused_shards(): pl.pallas_call(functools.partial(exchange_kernel, full), out_shape=tuple(...  52.7 us
    pallas_call x1, Pallas kernels, fused_shards(): pl.pallas_call(write_kernel, out_shape=kept, in_specs=[vmem] * 4, out_spe...  2.42 us

profile of v1, /device:TPU:0, one launch (start us, length us, event | category | flops | bytes accessed | tf_op | source)
XLA Modules:
  0.0 55.8 jit_solution(17409514083482228297)
XLA Ops:
  0.6 52.7 %shard_map.84 = (bf16[144,128]{1,0:T(8,128)(2,1)S(1)}, f32[1,144]{1,0:T(1,128)S(1)}, bf16[1152,1152]{1,0:T(8,128)(2,1)S(1)}, bf16[1152,1152]{1,0:T(8,128)(2,1)S(1)}) custom-call(bf16[576,128]{1,0:T(8,128)(2,1)} %bitcast.4, f32[18,128]{1,0:T(8,128)} %bitcast.5, bf16[128,1152]{1,0:T(8,128)(2,1)} %back_hbm.1, bf16[1152,1152]{1,0:T(8,128)(2,1)} %wg_hbm.1, ...), custom_call_target="tpu_custom_call" | custom-call | tf_op jit(solution)/shard_map/pallas_call | solution.py:555
  53.4 2.4 %shard_map.85 = (bf16[144,128]{1,0:T(8,128)(2,1)}, f32[1,144]{1,0:T(1,128)}, bf16[1152,1152]{1,0:T(8,128)(2,1)}, bf16[1152,1152]{1,0:T(8,128)(2,1)}) custom-call(bf16[144,128]{1,0:T(8,128)(2,1)S(1)} %get-tuple-element.12.grad_t, f32[1,144]{1,0:T(1,128)S(1)} %get-tuple-element.13.gain, bf16[1152,1152]{1,0:T(8,128)(2,1)S(1)} %get-tuple-element.14.grad_gate, ...), custom_call_target="tpu_custom_call" | custom-call | tf_op jit(solution)/shard_map/pallas_call | solution.py:618

commit v2 on v1

v2 whole, which is shorter than its diff:
```python
import functools

import jax
import jax.numpy as jnp
from jax import lax
from jax.experimental import pallas as pl
from jax.experimental.pallas import tpu as pltpu
from jax.sharding import PartitionSpec as P

D = 2304


epsilon = 1e-06


def gated_unit(gate, up):
    return jax.nn.gelu(gate, approximate=True) * up


def shards(tokens, hidden_grad, norm_gain, w_gate, w_up):
    n_dp = lax.axis_size("dp")
    n_model = lax.axis_size(("tp", "section"))
    rows_in = lax.all_gather(tokens, "section", axis=1, tiled=True)
    inputs = rows_in.astype(jnp.float32)
    inv_rms = lax.rsqrt(jnp.mean(inputs * inputs, axis=1) + epsilon)
    normed = (inputs * inv_rms[:, None] * norm_gain).astype(jnp.bfloat16)
    per_device, features = normed.shape
    cols_normed = lax.all_to_all(normed, "dp", split_axis=1, concat_axis=0, tiled=True)
    width = w_gate.shape[1]
    part_gate = jnp.dot(cols_normed, w_gate, preferred_element_type=jnp.float32)
    part_up = jnp.dot(cols_normed, w_up, preferred_element_type=jnp.float32)
    parts = jnp.concatenate([part_gate, part_up], axis=1).astype(jnp.bfloat16)
    parts = lax.all_to_all(parts, "dp", split_axis=0, concat_axis=0, tiled=True)
    sums = jnp.sum(parts.reshape(n_dp, per_device, 2 * width).astype(jnp.float32), axis=0)
    gate, up = sums[:, :width], sums[:, width:]
    hidden, pull = jax.vjp(gated_unit, gate, up)
    d_both = jnp.concatenate(pull(hidden_grad.astype(jnp.float32)), axis=1).astype(jnp.bfloat16)
    d_all = lax.all_gather(d_both, "dp", axis=0, tiled=True)
    d_gate, d_up = d_all[:, :width], d_all[:, width:]
    contract_cols = (((1,), (1,)), ((), ()))
    contract_rows = (((0,), (0,)), ((), ()))
    first = lax.dot_general(w_gate, d_gate, contract_cols, preferred_element_type=jnp.float32)
    second = lax.dot_general(w_up, d_up, contract_cols, preferred_element_type=jnp.float32)
    own_width = features // n_model
    per_row = n_model // n_dp
    d_part = (first + second).astype(jnp.bfloat16)
    d_part = d_part.reshape(per_row, own_width, n_dp, per_device).transpose(2, 0, 1, 3)
    d_part = d_part.reshape(n_model * own_width, per_device)
    d_columns = lax.psum_scatter(d_part, ("tp", "section"), scatter_dimension=0, tiled=True)
    moves = [
        (i * n_model + o * per_row + r, o * n_model + i * per_row + r)
        for i in range(n_dp)
        for o in range(n_dp)
        for r in range(per_row)
    ]
    d_columns = lax.ppermute(d_columns, ("dp", "tp", "section"), moves)
    d_normed = d_columns.astype(jnp.float32).T
    offset = lax.axis_index(("tp", "section")) * own_width
    own_inputs = lax.dynamic_slice_in_dim(inputs, offset, own_width, 1)
    own_gain = lax.dynamic_slice_in_dim(norm_gain, offset, own_width, 0)
    gain_part = jnp.sum(d_normed * own_inputs * inv_rms[:, None], axis=0)
    row_part = jnp.sum(own_inputs * own_gain * d_normed, axis=1)
    grad_gain = lax.psum(gain_part, "dp")
    row_sum = lax.psum(row_part, ("tp", "section"))
    grad_tokens = (
        inv_rms[:, None] * own_gain * d_normed
        - own_inputs * (inv_rms**3 * row_sum / features)[:, None]
    )
    grad_gate = lax.dot_general(cols_normed, d_gate, contract_rows, preferred_element_type=jnp.float32)
    grad_up = lax.dot_general(cols_normed, d_up, contract_rows, preferred_element_type=jnp.float32)
    return (
        grad_tokens.astype(jnp.bfloat16),
        grad_gain,
        grad_gate.astype(jnp.bfloat16),
        grad_up.astype(jnp.bfloat16),
    )


MESH = pl.DeviceIdType.MESH
SQRT_2_OVER_PI = 0.7978845608028654
CUBIC = 0.044715
CHUNKS = 3
HALVES = 2
CONTRACT_COLS = (((1,), (1,)), ((), ()))


def exchange_kernel(
    full,
    x_hbm,
    gain_hbm,
    back_hbm,
    wg_hbm,
    wu_hbm,
    grad_t,
    gain_out,
    grad_gate,
    grad_up,
    x_in,
    folded,
    gain_in,
    gain_col,
    w,
    back,
    relay,
    landed,
    xg,
    xs,
    xn,
    slab,
    squares,
    part_send,
    part_recv,
    own_part,
    d_all,
    own_pieces,
    own_sib,
    own_halved,
    own_incoming,
    pieces,
    sib_in,
    halved,
    incoming,
    move_send,
    moved,
    rows,
    prods,
    gains,
    far,
    load_sem,
    w_sem,
    tok_send,
    a_recv,
    b_recv,
    relay_recv,
    own_recv,
    core_send,
    core_recv,
    slab_sem,
    sq_sem,
    part_ssem,
    part_rsem,
    d_ssem,
    d_rsem,
    piece_ssem,
    piece_rsem,
    sib_ssem,
    sib_rsem,
    last_send,
    last_recv,
    row_sem,
):
    i, t, s = lax.axis_index("dp"), lax.axis_index("tp"), lax.axis_index("section")
    other = 1 - i
    f32, bf = jnp.float32, jnp.bfloat16
    sec_rows, per_device = x_in.shape
    own = slab.shape[0]
    block = 2 * sec_rows
    half, q = s // 2, lax.rem(s, 2)
    sibling, across = s + 1 - 2 * q, s + 2 - 4 * half
    ck = w.shape[2] // 2
    th = per_device // HALVES
    fold = own // 2
    flat = sec_rows // 2
    cut = flat // 2
    reducer = t // 2 == i
    not_reducer = jnp.logical_not(reducer)

    def to(d, tt, ss):
        return {"dp": d, "tp": tt, "section": ss}

    def send(src, dst, ssem, rsem, target):
        return pltpu.make_async_remote_copy(
            src_ref=src, dst_ref=dst, send_sem=ssem, recv_sem=rsem, device_id=target, device_id_type=MESH
        )

    xdev, ydev, cdev = to(other, t, s), to(i, t, across), to(i, t, sibling)

    def sent(ref, ssem):
        send(ref, ref, ssem, load_sem.at[0], xdev).wait_send()

    def received(ref, rsem):
        send(ref, ref, load_sem.at[0], rsem, xdev).wait_recv()

    barrier = pltpu.get_barrier_semaphore()
    near = [to(i, t, lax.rem(s + ds, 4)) for ds in range(1, 4)] + [xdev]
    z_near = 1 + (lax.rem(t, 3) + 2) // 3

    def signal_z(sem):
        @pl.when(t < 3)
        def _():
            pl.semaphore_signal(sem, inc=1, device_id=to(i, t + 1, s), device_id_type=MESH)

        @pl.when(t > 0)
        def _():
            pl.semaphore_signal(sem, inc=1, device_id=to(i, t - 1, s), device_id_type=MESH)

    x_load = pltpu.make_async_copy(x_hbm, x_in, load_sem.at[0])
    x_load.start()
    for target in near:
        pl.semaphore_signal(barrier, inc=1, device_id=target, device_id_type=MESH)
    signal_z(barrier)

    gain_load = pltpu.make_async_copy(gain_hbm, gain_in, load_sem.at[1])
    back_load = pltpu.make_async_copy(back_hbm, back, load_sem.at[2])
    loads = []
    for k in range(CHUNKS):
        cols = pl.ds(k * ck, ck)
        loads.append(
            (
                pltpu.make_async_copy(wg_hbm.at[:, cols], w.at[k, :, pl.ds(0, ck)], w_sem.at[0, k]),
                pltpu.make_async_copy(wu_hbm.at[:, cols], w.at[k, :, pl.ds(ck, ck)], w_sem.at[1, k]),
            )
        )

    def mine_at(n):
        return pl.ds(pl.multiple_of(q * flat + n * cut, 16), cut)

    my_rows = pl.ds(pl.multiple_of(q * sec_rows, 16), sec_rows)
    first, second = pl.ds(0, cut), pl.ds(cut, cut)
    x_first, x_second, y_second, y_first, x_relay, core_first, core_second, y_own = ([] for _ in range(8))
    for h in range(HALVES):
        a_here, b_here = landed.at[h, mine_at(0)], landed.at[h, mine_at(1)]
        x_first.append(send(folded.at[h, first], a_here, tok_send.at[0], a_recv.at[h], xdev))
        x_second.append(send(folded.at[h, second], b_here, tok_send.at[0], b_recv.at[h], xdev))
        y_second.append(send(folded.at[h, second], relay.at[h], tok_send.at[1], relay_recv.at[h], ydev))
        y_first.append(send(a_here, a_here, tok_send.at[1], a_recv.at[h], ydev))
        x_relay.append(send(relay.at[h], b_here, tok_send.at[2], b_recv.at[h], xdev))
        core_first.append(send(a_here, a_here, core_send.at[0], core_recv.at[h], cdev))
        core_second.append(send(b_here, b_here, core_send.at[0], core_recv.at[h], cdev))
        part = pl.ds(h * flat, flat)
        there = pl.ds(pl.multiple_of(q * sec_rows + h * flat, 16), flat)
        y_own.append(send(x_in.at[part], xg.at[0, there], tok_send.at[0], own_recv.at[h], ydev))
    core_own_in = send(x_in, xg.at[0, my_rows], core_send.at[1], core_recv.at[HALVES], cdev)
    core_own = send(xg.at[0, my_rows], xg.at[0, my_rows], core_send.at[1], core_recv.at[HALVES], cdev)
    left = lax.broadcasted_iota(jnp.int32, (flat, per_device), 1) < th
    left_own = lax.broadcasted_iota(jnp.int32, (fold, per_device), 1) < th

    x_load.wait()
    gain_load.start()
    for load in loads[0]:
        load.start()
    back_load.start()
    for k in range(1, CHUNKS):
        for load in loads[k]:
            load.start()
    raw = x_in[...].astype(f32)
    upper, lower = raw[:flat], raw[flat:]
    folded[0] = jnp.where(left, upper, pltpu.roll(lower, th, 1)).astype(bf)
    folded[1] = jnp.where(left, pltpu.roll(upper, th, 1), lower).astype(bf)
    squares[0] = jnp.broadcast_to(jnp.sum(raw * raw, axis=0, keepdims=True), squares.shape[1:])

    pl.semaphore_wait(barrier, len(near) + z_near)

    @pl.when(half != i)
    def _():
        for h in range(HALVES):
            x_first[h].start()
            y_second[h].start()
            x_second[h].start()

    @pl.when(half == i)
    def _():
        y_own[0].start()
        core_own_in.start()
        xg[0, my_rows] = x_in[...]

    signal_z(far.at[0])
    for ds in range(1, 4):
        send(squares.at[0], squares.at[ds], sq_sem.at[0], sq_sem.at[1], to(i, t, lax.rem(s + ds, 4))).start()

    gain_load.wait()
    n_rows = gain_in.shape[0]
    filled = jnp.concatenate([gain_in[...], jnp.zeros((128 - n_rows, 128), f32)], axis=0).T
    for b in range(n_rows):
        gain_col[b * 128 : (b + 1) * 128] = jnp.broadcast_to(filled[:, b : b + 1], (128, 128))

    @pl.when(half == i)
    def _():
        for h in range(HALVES):
            x_first[h].wait_recv()
            y_first[h].start()
            core_first[h].start()
            y_second[h].wait_recv()
            x_relay[h].start()
            if h == 0:
                y_own[1].start()
            x_second[h].wait_recv()
            core_second[h].start()

    @pl.when(half != i)
    def _():
        x_relay[0].wait_recv()
        core_second[0].start()
        y_first[0].wait_recv()
        core_first[0].start()

    half_gain = gain_col.at[pl.ds(pl.multiple_of(i * block, 16), block)]

    def unfold(h):
        sections = []
        for c in range(2):
            values = landed[h, c * flat : (c + 1) * flat].astype(f32)
            turned = pltpu.roll(values, th, 1)
            sections += [values, turned] if h == 0 else [turned, values]
        fresh = jnp.concatenate(sections, axis=0)
        if h > 0:
            wide = lax.broadcasted_iota(jnp.int32, fresh.shape, 1) < th
            fresh = jnp.where(wide, xg[1].astype(f32), fresh)
        xg[1] = fresh.astype(bf)
        scaled = (fresh * half_gain[...]).astype(bf)
        if h > 0:
            xs[:, per_device : 2 * per_device] = scaled
        xn[1, h * th : (h + 1) * th] = scaled.T[h * th : (h + 1) * th]

    part_sends, d_sends = {}, {}
    for h in range(HALVES):
        if h > 0:

            @pl.when(half != i)
            def _(h=h):
                x_relay[h].wait_recv()
                core_second[h].start()
                y_first[h].wait_recv()
                core_first[h].start()
                y_own[0].wait_recv()
                y_own[1].wait_recv()
                core_own.start()

        received(landed.at[h, pl.ds(0, flat)], core_recv.at[h])
        unfold(h)
        for k in range(CHUNKS):
            if h == 0:
                for load in loads[k]:
                    load.wait()
            part_send[h, k] = jnp.dot(
                xn[1, h * th : (h + 1) * th], w[k], preferred_element_type=f32
            ).astype(bf)
            copy = send(part_send.at[h, k], part_recv.at[h, k], part_ssem, part_rsem.at[h, k], xdev)
            copy.start()
            part_sends[h, k] = copy

    @pl.when(s == t)
    def _():
        for ds in range(1, 4):
            ss = lax.rem(s + ds, 4)
            there = pl.ds(pl.multiple_of(ss * own, 16), own)
            send(x_in.at[there], slab, slab_sem.at[0], slab_sem.at[1], to(i, t, ss)).start()
        slab[...] = x_in[pl.ds(pl.multiple_of(s * own, 16), own)]

    pl.semaphore_wait(far.at[0], z_near)
    signal_z(far.at[1])
    core_own.wait_recv()
    scaled = (xg[0].astype(f32) * half_gain[...]).astype(bf)
    xs[:, :per_device] = scaled
    xn[0] = scaled.T
    for k in range(CHUNKS):
        own_part[k] = jnp.dot(xn[0], w[k], preferred_element_type=f32)
    pl.semaphore_wait(far.at[1], z_near)
    signal_z(far.at[2])
    received(squares.at[pl.ds(1, 3)], sq_sem.at[1])
    total = squares[0] + squares[1] + squares[2] + squares[3]
    inv_row = lax.rsqrt(total[:1] / full + epsilon)
    inv_all = jnp.broadcast_to(inv_row, (per_device, per_device)).T[:, :1]
    back_load.wait()

    row_cols = []
    for h in range(HALVES):
        here = slice(h * th, (h + 1) * th)
        inv = inv_all[here]
        row_col = jnp.zeros((th, 1), f32)
        for k in range(CHUNKS):
            part_sends[h, k].wait_recv()
            raw_sums = own_part[k, here] + part_recv[h, k].astype(f32)
            gate, up = raw_sums[:, :ck] * inv, raw_sums[:, ck:] * inv
            grad = back[here, k * ck : (k + 1) * ck].astype(f32) * inv
            square = gate * gate
            tanh = jnp.tanh(SQRT_2_OVER_PI * gate * (1.0 + CUBIC * square))
            cdf = 0.5 * (1.0 + tanh)
            slope = cdf + 0.5 * gate * (1.0 - tanh * tanh) * (SQRT_2_OVER_PI * (1.0 + 3.0 * CUBIC * square))
            d_gate, d_up = grad * up * slope, grad * gate * cdf
            d_all[0, k, here, pl.ds(0, ck)] = d_gate.astype(bf)
            d_all[0, k, here, pl.ds(ck, ck)] = d_up.astype(bf)
            these = pl.ds(h * th, th)
            copy = send(d_all.at[0, k, these], d_all.at[1, k, these], d_ssem, d_rsem.at[h, k], xdev)
            copy.start()
            d_sends[h, k] = copy
            terms = d_gate * raw_sums[:, :ck] + d_up * raw_sums[:, ck:]
            row_col = row_col + jnp.sum(terms, axis=1, keepdims=True)
        row_cols.append(row_col)

    row_col = jnp.concatenate(row_cols, axis=0)
    rows[0] = jnp.broadcast_to(row_col, (per_device, per_device)).T[:8]
    pl.semaphore_wait(far.at[2], z_near)
    for dt in range(4):
        for ds in range(4):
            if dt + ds > 0:
                target = to(i, lax.rem(t + dt, 4), lax.rem(s + ds, 4))
                send(rows.at[0], rows.at[dt * 4 + ds], row_sem.at[0], row_sem.at[1], target).start()

    def scatter(parts, landing, n):
        for e in (1, 0):
            tt = 2 * i + lax.rem(t + e, 2)
            dt = lax.rem(tt - t + 4, 4)
            for dy in (1, 0):
                ss = across if dy else s
                r = lax.rem(tt, 2) * 2 + ss // 2
                slot = dt * 2 + dy
                copy = send(parts.at[r], landing.at[slot], piece_ssem.at[n], piece_rsem.at[n], to(i, tt, ss))
                if e == 0 and dy == 0:

                    @pl.when(reducer)
                    def _(r=r):
                        landing[0] = parts[r]

                    @pl.when(not_reducer)
                    def _(copy=copy):
                        copy.start()

                else:
                    copy.start()

    def scattered(parts, n):
        @pl.when(reducer)
        def _():
            sent(parts.at[pl.ds(0, 3)], piece_ssem.at[n])

        @pl.when(not_reducer)
        def _():
            sent(parts, piece_ssem.at[n])

    def gathered(landing, n):
        received(landing.at[pl.ds(1, 7)], piece_rsem.at[n])
        result = landing[0].astype(f32)
        for slot in range(1, 8):
            result = result + landing[slot].astype(f32)
        return result

    acc = None
    for k in range(CHUNKS):
        term = lax.dot_general(w[k], d_all[0, k], CONTRACT_COLS, preferred_element_type=f32)
        acc = term if acc is None else acc + term
    for r in range(8):
        own_pieces[r % 2, r // 2] = acc[r * own : (r + 1) * own].astype(bf)
    own_swap = send(own_pieces.at[1 - q], own_sib, sib_ssem.at[HALVES], sib_rsem.at[HALVES], cdev)
    own_swap.start()
    own_swap.wait_recv()
    own_halved[...] = (own_pieces[q].astype(f32) + own_sib[...].astype(f32)).astype(bf)
    scatter(own_halved, own_incoming, HALVES)

    def weight_grads(k):
        both = jnp.concatenate([d_all[0, k], d_all[1, k]], axis=0)
        cols = pl.ds(k * ck, ck)
        grads = jnp.dot(xs[...], both, preferred_element_type=f32).astype(bf)
        grad_gate[:, cols] = grads[:, :ck]
        grad_up[:, cols] = grads[:, ck:]

    swaps = []
    for h in range(HALVES):
        acc = None
        for k in range(CHUNKS):
            d_sends[h, k].wait_recv()
            late = d_all[1, k, h * th : (h + 1) * th]
            twice = jnp.concatenate([late, late], axis=0)
            term = lax.dot_general(w[k], twice, CONTRACT_COLS, preferred_element_type=f32)
            acc = term if acc is None else acc + term
            if h == HALVES - 1 and k == 0:
                weight_grads(0)
        for r in range(8):
            top, bottom = acc[r * own : r * own + fold], acc[r * own + fold : (r + 1) * own]
            pieces[h, r % 2, r // 2] = jnp.where(left_own, top, bottom).astype(bf)
        swap = send(pieces.at[h, 1 - q], sib_in.at[h], sib_ssem.at[h], sib_rsem.at[h], cdev)
        swap.start()
        if h == HALVES - 1:
            weight_grads(1)
        swap.wait_recv()
        swaps.append(swap)
        halved[h] = (pieces[h, q].astype(f32) + sib_in[h].astype(f32)).astype(bf)
        scatter(halved.at[h], incoming.at[h], h)

    weight_grads(CHUNKS - 1)
    received(rows.at[pl.ds(1, 15)], row_sem.at[1])
    row_sum = rows[0]
    for slot in range(1, 16):
        row_sum = row_sum + rows[slot]
    factor = inv_row * inv_row * row_sum[:1] / full

    @pl.when(s != t)
    def _():
        received(slab, slab_sem.at[1])

    mine = slab[...].astype(f32)
    gain_own = gain_col[pl.ds(pl.multiple_of((t * 4 + s) * own, 16), own)]

    def moves(h):
        return send(move_send.at[h], moved.at[h], last_send.at[0], last_recv.at[h], xdev)

    gain_copy = send(gains.at[0], gains.at[1], last_send.at[1], last_recv.at[HALVES], xdev)

    @pl.when(reducer)
    def _():
        d_own = gathered(own_incoming, HALVES)
        grad_t[...] = (gain_own * d_own - mine * factor).astype(bf)
        prods[pl.ds(0, own)] = mine * d_own
        prods[pl.ds(own, prods.shape[0] - own)] = jnp.zeros((prods.shape[0] - own, per_device), f32)
        local = pl.multiple_of((lax.rem(t, 2) * 4 + s) * own, 16)
        theirs = xg[1, pl.ds(local, own)].astype(f32)
        top, bottom = theirs[:fold], theirs[fold:]
        for h in range(HALVES):
            d_late = gathered(incoming.at[h], h)
            move_send[h] = d_late.astype(bf)
            moves(h).start()
            if h == 0:
                match = jnp.where(left_own, top, pltpu.roll(bottom, th, 1))
            else:
                match = jnp.where(left_own, pltpu.roll(top, th, 1), bottom)
            product = d_late * match
            prods[pl.ds(0, fold)] += jnp.where(left_own, product, 0.0)
            prods[pl.ds(fold, fold)] += jnp.where(left_own, 0.0, product)
        gains[0] = jnp.broadcast_to(jnp.sum(prods[...].T, axis=0, keepdims=True), gains.shape[1:])
        gain_copy.start()
        gain_out[...] = gains[0, :1, :own]

    def drain():
        @pl.when(half != i)
        def _():
            sent(folded, tok_send.at[0])
            sent(relay, tok_send.at[1])

        @pl.when(half == i)
        def _():
            sent(x_in, tok_send.at[0])
            sent(relay, tok_send.at[1])
            sent(relay, tok_send.at[2])

        sent(folded, core_send.at[0])
        sent(x_in, core_send.at[1])

        @pl.when(s == t)
        def _():
            sent(x_in.at[pl.ds(0, 3 * own)], slab_sem.at[0])

        sent(squares.at[pl.ds(1, 3)], sq_sem.at[0])
        sent(part_send, part_ssem)
        sent(d_all.at[0], d_ssem)
        sent(rows.at[pl.ds(1, 15)], row_sem.at[0])
        for copy in [own_swap] + swaps:
            copy.wait_send()
        scattered(own_halved, HALVES)
        for h in range(HALVES):
            scattered(halved.at[h], h)

    drain()

    @pl.when(reducer)
    def _():
        sent(move_send, last_send.at[0])
        gain_copy.wait_send()

    @pl.when(not_reducer)
    def _():
        moves(0).wait_recv()
        moves(1).wait_recv()
        early, final = moved[0].astype(f32), moved[1].astype(f32)
        top = jnp.where(left_own, early, pltpu.roll(final, th, 1))
        bottom = jnp.where(left_own, pltpu.roll(early, th, 1), final)
        grad_t[...] = (gain_own * jnp.concatenate([top, bottom], axis=0) - mine * factor).astype(bf)
        gain_copy.wait_recv()
        gain_out[...] = gains[1, :1, :own]


WRITES = 4


def write_kernel(grad_t, gain, grad_gate, grad_up, grad_t_out, gain_out, gate_out, up_out, sems):
    pairs = [(grad_t, grad_t_out), (gain, gain_out)]
    n = grad_gate.shape[0] // WRITES
    for p in range(WRITES):
        part = pl.ds(p * n, n)
        pairs += [(grad_gate.at[part], gate_out.at[part]), (grad_up.at[part], up_out.at[part])]
    copies = [pltpu.make_async_copy(src, dst, sems.at[n]) for n, (src, dst) in enumerate(pairs)]
    for copy in copies:
        copy.start()
    for copy in copies:
        copy.wait()


def fused_shards(tokens, hidden_grad, norm_gain, w_gate, w_up):
    per_device, sec_rows = tokens.shape
    block, width = w_gate.shape
    full = norm_gain.shape[0]
    own = full // 16
    ck = width // CHUNKS
    th = per_device // HALVES
    fold = own // 2
    flat = sec_rows // 2
    bf, f32 = jnp.bfloat16, jnp.float32
    vmem = pl.BlockSpec(memory_space=pltpu.VMEM)
    anywhere = pl.BlockSpec(memory_space=pltpu.HBM)
    dma = pltpu.SemaphoreType.DMA
    own_pad = pl.cdiv(own, 128) * 128
    kept = (
        jax.ShapeDtypeStruct((own, per_device), bf),
        jax.ShapeDtypeStruct((1, own), f32),
        jax.ShapeDtypeStruct((block, width), bf),
        jax.ShapeDtypeStruct((block, width), bf),
    )
    operands = (tokens.T, norm_gain.reshape(full // 128, 128), hidden_grad, w_gate, w_up)
    results = pl.pallas_call(
        functools.partial(exchange_kernel, full),
        out_shape=tuple(pltpu.VMEM(a.shape, a.dtype) for a in kept),
        in_specs=[anywhere] * 5,
        out_specs=(vmem,) * 4,
        scratch_shapes=[
            pltpu.VMEM((sec_rows, per_device), bf),
            pltpu.VMEM((HALVES, flat, per_device), bf),
            pltpu.VMEM((full // 128, 128), f32),
            pltpu.VMEM((full, 128), f32),
            pltpu.VMEM((CHUNKS, block, 2 * ck), bf),
            pltpu.VMEM((per_device, width), bf),
            pltpu.VMEM((HALVES, flat // 2, per_device), bf),
            pltpu.VMEM((HALVES, 2 * flat, per_device), bf),
            pltpu.VMEM((2, block, per_device), bf),
            pltpu.VMEM((block, 2 * per_device), bf),
            pltpu.VMEM((2, per_device, block), bf),
            pltpu.VMEM((own, per_device), bf),
            pltpu.VMEM((4, 8, per_device), f32),
            pltpu.VMEM((HALVES, CHUNKS, th, 2 * ck), bf),
            pltpu.VMEM((HALVES, CHUNKS, th, 2 * ck), bf),
            pltpu.VMEM((CHUNKS, per_device, 2 * ck), f32),
            pltpu.VMEM((2, CHUNKS, per_device, 2 * ck), bf),
            pltpu.VMEM((2, 4, own, per_device), bf),
            pltpu.VMEM((4, own, per_device), bf),
            pltpu.VMEM((4, own, per_device), bf),
            pltpu.VMEM((8, own, per_device), bf),
            pltpu.VMEM((HALVES, 2, 4, fold, per_device), bf),
            pltpu.VMEM((HALVES, 4, fold, per_device), bf),
            pltpu.VMEM((HALVES, 4, fold, per_device), bf),
            pltpu.VMEM((HALVES, 8, fold, per_device), bf),
            pltpu.VMEM((HALVES, fold, per_device), bf),
            pltpu.VMEM((HALVES, fold, per_device), bf),
            pltpu.VMEM((16, 8, per_device), f32),
            pltpu.VMEM((own_pad, per_device), f32),
            pltpu.VMEM((2, 8, own_pad), f32),
            pltpu.SemaphoreType.REGULAR((3,)),
            dma((3,)),
            dma((2, CHUNKS)),
            dma((3,)),
            dma((HALVES,)),
            dma((HALVES,)),
            dma((HALVES,)),
            dma((HALVES,)),
            dma((2,)),
            dma((HALVES + 1,)),
            dma((2,)),
            dma((2,)),
            dma,
            dma((HALVES, CHUNKS)),
            dma,
            dma((HALVES, CHUNKS)),
            dma((HALVES + 1,)),
            dma((HALVES + 1,)),
            dma((HALVES + 1,)),
            dma((HALVES + 1,)),
            dma((2,)),
            dma((HALVES + 1,)),
            dma((2,)),
        ],
        compiler_params=pltpu.CompilerParams(
            collective_id=0, has_side_effects=True, vmem_limit_bytes=40 * 1024 * 1024
        ),
    )(*(pltpu.with_memory_space_constraint(a, pltpu.HBM) for a in operands))
    grad_t, gain, grad_gate, grad_up = pl.pallas_call(
        write_kernel,
        out_shape=kept,
        in_specs=[vmem] * 4,
        out_specs=(anywhere,) * 4,
        scratch_shapes=[dma((2 * WRITES + 2,))],
        compiler_params=pltpu.CompilerParams(vmem_limit_bytes=16 * 1024 * 1024),
    )(*results)
    return grad_t.T, gain.reshape(own), grad_gate, grad_up


def solution(mesh):
    in_specs = (
        P("dp", "section"),
        P("dp", ("tp", "section")),
        P(),
        P("dp", ("tp", "section")),
        P("dp", ("tp", "section")),
    )
    out_specs = (
        P("dp", ("tp", "section")),
        P(("tp", "section")),
        P("dp", ("tp", "section")),
        P("dp", ("tp", "section")),
    )
    sizes = tuple(mesh.shape[a] for a in ("dp", "tp", "section"))
    body = fused_shards if sizes == (2, 4, 4) else shards
    return jax.shard_map(body, mesh=mesh, in_specs=in_specs, out_specs=out_specs, check_vma=False)
```

time: 55.9 us -> 53.2 us (0.952)
  Pallas kernels: 55.1 us -> 52.4 us
    pallas_call x1, Pallas kernels: 52.7 us -> 49.9 us  [fused_shards(): pl.pallas_call(functools.partial(exchange_kernel, full), out_shape=tuple(...]
where the time goes in v2:
time: 53.2 us; the launch traced here: 53 us
  Pallas kernels  52.4 us (98%)
  between operations  0.64 us (1%)
    pallas_call x1, Pallas kernels, fused_shards(): pl.pallas_call(functools.partial(exchange_kernel, full), out_shape=tuple(...  49.9 us
    pallas_call x1, Pallas kernels, fused_shards(): pl.pallas_call(write_kernel, out_shape=kept, in_specs=[vmem] * 4, out_spe...  2.47 us

profile of v2, /device:TPU:0, one launch (start us, length us, event | category | flops | bytes accessed | tf_op | source)
XLA Modules:
  0.0 53.0 jit_solution(11156068892091327366)
XLA Ops:
  0.6 49.9 %shard_map.84 = (bf16[144,128]{1,0:T(8,128)(2,1)S(1)}, f32[1,144]{1,0:T(1,128)S(1)}, bf16[1152,1152]{1,0:T(8,128)(2,1)S(1)}, bf16[1152,1152]{1,0:T(8,128)(2,1)S(1)}) custom-call(bf16[576,128]{1,0:T(8,128)(2,1)} %bitcast.4, f32[18,128]{1,0:T(8,128)} %bitcast.5, bf16[128,1152]{1,0:T(8,128)(2,1)} %back_hbm.1, bf16[1152,1152]{1,0:T(8,128)(2,1)} %wg_hbm.1, ...), custom_call_target="tpu_custom_call" | custom-call | tf_op jit(solution)/shard_map/pallas_call | solution.py:608
  50.6 2.5 %shard_map.85 = (bf16[144,128]{1,0:T(8,128)(2,1)}, f32[1,144]{1,0:T(1,128)}, bf16[1152,1152]{1,0:T(8,128)(2,1)}, bf16[1152,1152]{1,0:T(8,128)(2,1)}) custom-call(bf16[144,128]{1,0:T(8,128)(2,1)S(1)} %get-tuple-element.12.grad_t, f32[1,144]{1,0:T(1,128)S(1)} %get-tuple-element.13.gain, bf16[1152,1152]{1,0:T(8,128)(2,1)S(1)} %get-tuple-element.14.grad_gate, ...), custom_call_target="tpu_custom_call" | custom-call | tf_op jit(solution)/shard_map/pallas_call | solution.py:672

commit v3 on v2

--- a/solution.py
+++ b/solution.py
@@ -80,8 +80,15 @@
 SQRT_2_OVER_PI = 0.7978845608028654
 CUBIC = 0.044715
 CHUNKS = 3
-HALVES = 2
-CONTRACT_COLS = (((1,), (1,)), ((), ()))
+SENT_GROUPS = ((0, 32), (32, 32), (64, 64))
+LATE_GROUPS = ((0, 64), (64, 32), (96, 32))
+
+
+def spans(own, ways):
+    tall = pl.cdiv(own // ways, 8) * 8
+    count = (own - ways * (tall - 8)) // 8
+    lengths = [tall if j < count else tall - 8 for j in range(ways)]
+    return [(sum(lengths[:j]), lengths[j]) for j in range(ways)]
 
 
 def exchange_kernel(
@@ -97,12 +104,12 @@
     grad_up,
     x_in,
     folded,
+    landed,
     gain_in,
     gain_col,
     w,
+    w_t,
     back,
-    relay,
-    landed,
     xg,
     xs,
     xn,
@@ -116,12 +123,7 @@
     own_sib,
     own_halved,
     own_incoming,
-    pieces,
-    sib_in,
-    halved,
-    incoming,
-    move_send,
-    moved,
+    late_bufs,
     rows,
     prods,
     gains,
@@ -129,10 +131,7 @@
     load_sem,
     w_sem,
     tok_send,
-    a_recv,
-    b_recv,
-    relay_recv,
-    own_recv,
+    tok_recv,
     core_send,
     core_recv,
     slab_sem,
@@ -158,10 +157,8 @@
     half, q = s // 2, lax.rem(s, 2)
     sibling, across = s + 1 - 2 * q, s + 2 - 4 * half
     ck = w.shape[2] // 2
-    th = per_device // HALVES
-    fold = own // 2
-    flat = sec_rows // 2
-    cut = flat // 2
+    n_sent, n_late = len(SENT_GROUPS), len(LATE_GROUPS)
+    lane = lax.broadcasted_iota(jnp.int32, (1, per_device), 1)
     reducer = t // 2 == i
     not_reducer = jnp.logical_not(reducer)
 
@@ -174,6 +171,17 @@
         )
 
     xdev, ydev, cdev = to(other, t, s), to(i, t, across), to(i, t, sibling)
+    diagonal = to(other, t, across)
+
+    def turn(value, shift):
+        shift = shift % per_device
+        return pltpu.roll(value, shift, 1) if shift else value
+
+    def pick(parts, size):
+        result = parts[0]
+        for j in range(1, len(parts)):
+            result = jnp.where(lane >= j * size, parts[j], result)
+        return result
 
     def sent(ref, ssem):
         send(ref, ref, ssem, load_sem.at[0], xdev).wait_send()
@@ -182,7 +190,7 @@
         send(ref, ref, load_sem.at[0], rsem, xdev).wait_recv()
 
     barrier = pltpu.get_barrier_semaphore()
-    near = [to(i, t, lax.rem(s + ds, 4)) for ds in range(1, 4)] + [xdev]
+    near = [to(i, t, lax.rem(s + ds, 4)) for ds in range(1, 4)] + [xdev, diagonal]
     z_near = 1 + (lax.rem(t, 3) + 2) // 3
 
     def signal_z(sem):
@@ -196,11 +204,12 @@
 
     x_load = pltpu.make_async_copy(x_hbm, x_in, load_sem.at[0])
     x_load.start()
+    gain_load = pltpu.make_async_copy(gain_hbm, gain_in, load_sem.at[1])
+    gain_load.start()
     for target in near:
         pl.semaphore_signal(barrier, inc=1, device_id=target, device_id_type=MESH)
     signal_z(barrier)
 
-    gain_load = pltpu.make_async_copy(gain_hbm, gain_in, load_sem.at[1])
     back_load = pltpu.make_async_copy(back_hbm, back, load_sem.at[2])
     loads = []
     for k in range(CHUNKS):
@@ -212,31 +221,19 @@
             )
         )
 
-    def mine_at(n):
-        return pl.ds(pl.multiple_of(q * flat + n * cut, 16), cut)
-
     my_rows = pl.ds(pl.multiple_of(q * sec_rows, 16), sec_rows)
-    first, second = pl.ds(0, cut), pl.ds(cut, cut)
-    x_first, x_second, y_second, y_first, x_relay, core_first, core_second, y_own = ([] for _ in range(8))
-    for h in range(HALVES):
-        a_here, b_here = landed.at[h, mine_at(0)], landed.at[h, mine_at(1)]
-        x_first.append(send(folded.at[h, first], a_here, tok_send.at[0], a_recv.at[h], xdev))
-        x_second.append(send(folded.at[h, second], b_here, tok_send.at[0], b_recv.at[h], xdev))
-        y_second.append(send(folded.at[h, second], relay.at[h], tok_send.at[1], relay_recv.at[h], ydev))
-        y_first.append(send(a_here, a_here, tok_send.at[1], a_recv.at[h], ydev))
-        x_relay.append(send(relay.at[h], b_here, tok_send.at[2], b_recv.at[h], xdev))
-        core_first.append(send(a_here, a_here, core_send.at[0], core_recv.at[h], cdev))
-        core_second.append(send(b_here, b_here, core_send.at[0], core_recv.at[h], cdev))
-        part = pl.ds(h * flat, flat)
-        there = pl.ds(pl.multiple_of(q * sec_rows + h * flat, 16), flat)
-        y_own.append(send(x_in.at[part], xg.at[0, there], tok_send.at[0], own_recv.at[h], ydev))
-    core_own_in = send(x_in, xg.at[0, my_rows], core_send.at[1], core_recv.at[HALVES], cdev)
-    core_own = send(xg.at[0, my_rows], xg.at[0, my_rows], core_send.at[1], core_recv.at[HALVES], cdev)
-    left = lax.broadcasted_iota(jnp.int32, (flat, per_device), 1) < th
-    left_own = lax.broadcasted_iota(jnp.int32, (fold, per_device), 1) < th
+    to_near, to_far, to_core = [], [], []
+    for g in range(n_sent):
+        n = folded[g].shape[0]
+        here = landed[g].at[pl.ds(pl.multiple_of(q * n, 16), n)]
+        to_near.append(send(folded[g], here, tok_send.at[0], tok_recv.at[g], xdev))
+        to_far.append(send(folded[g], here, tok_send.at[1], tok_recv.at[g], diagonal))
+        to_core.append(send(here, here, core_send.at[0], core_recv.at[g], cdev))
+    y_own = send(x_in, xg.at[0, my_rows], tok_send.at[0], tok_recv.at[n_sent], ydev)
+    core_own_in = send(x_in, xg.at[0, my_rows], core_send.at[1], core_recv.at[n_sent], cdev)
+    core_own = send(xg.at[0, my_rows], xg.at[0, my_rows], core_send.at[1], core_recv.at[n_sent], cdev)
 
     x_load.wait()
-    gain_load.start()
     for load in loads[0]:
         load.start()
     back_load.start()
@@ -244,23 +241,23 @@
         for load in loads[k]:
             load.start()
     raw = x_in[...].astype(f32)
-    upper, lower = raw[:flat], raw[flat:]
-    folded[0] = jnp.where(left, upper, pltpu.roll(lower, th, 1)).astype(bf)
-    folded[1] = jnp.where(left, pltpu.roll(upper, th, 1), lower).astype(bf)
+    for g, (start, size) in enumerate(SENT_GROUPS):
+        n = folded[g].shape[0]
+        ways = per_device // size
+        parts = [turn(raw[j * n : (j + 1) * n], j * size - start) for j in range(ways)]
+        folded[g][...] = pick(parts, size).astype(bf)
     squares[0] = jnp.broadcast_to(jnp.sum(raw * raw, axis=0, keepdims=True), squares.shape[1:])
 
     pl.semaphore_wait(barrier, len(near) + z_near)
 
     @pl.when(half != i)
     def _():
-        for h in range(HALVES):
-            x_first[h].start()
-            y_second[h].start()
-            x_second[h].start()
+        for g in range(n_sent):
+            to_far[g].start()
+            to_near[g].start()
 
     @pl.when(half == i)
     def _():
-        y_own[0].start()
         core_own_in.start()
         xg[0, my_rows] = x_in[...]
 
@@ -274,70 +271,59 @@
     for b in range(n_rows):
         gain_col[b * 128 : (b + 1) * 128] = jnp.broadcast_to(filled[:, b : b + 1], (128, 128))
 
-    @pl.when(half == i)
-    def _():
-        for h in range(HALVES):
-            x_first[h].wait_recv()
-            y_first[h].start()
-            core_first[h].start()
-            y_second[h].wait_recv()
-            x_relay[h].start()
-            if h == 0:
-                y_own[1].start()
-            x_second[h].wait_recv()
-            core_second[h].start()
-
-    @pl.when(half != i)
-    def _():
-        x_relay[0].wait_recv()
-        core_second[0].start()
-        y_first[0].wait_recv()
-        core_first[0].start()
+    for k in range(CHUNKS):
+        for load in loads[k]:
+            load.wait()
+        w_t[k] = w[k].T
 
     half_gain = gain_col.at[pl.ds(pl.multiple_of(i * block, 16), block)]
 
-    def unfold(h):
-        sections = []
+    def unfold(g):
+        start, size = SENT_GROUPS[g]
+        n = folded[g].shape[0]
+        parts = []
         for c in range(2):
-            values = landed[h, c * flat : (c + 1) * flat].astype(f32)
-            turned = pltpu.roll(values, th, 1)
-            sections += [values, turned] if h == 0 else [turned, values]
-        fresh = jnp.concatenate(sections, axis=0)
-        if h > 0:
-            wide = lax.broadcasted_iota(jnp.int32, fresh.shape, 1) < th
-            fresh = jnp.where(wide, xg[1].astype(f32), fresh)
+            values = landed[g][c * n : (c + 1) * n].astype(f32)
+            parts += [turn(values, start - j * size) for j in range(per_device // size)]
+        fresh = jnp.concatenate(parts, axis=0)
+        if g > 0:
+            fresh = jnp.where(lane >= start, fresh, xg[1].astype(f32))
         xg[1] = fresh.astype(bf)
         scaled = (fresh * half_gain[...]).astype(bf)
-        if h > 0:
+        if g == n_sent - 1:
             xs[:, per_device : 2 * per_device] = scaled
-        xn[1, h * th : (h + 1) * th] = scaled.T[h * th : (h + 1) * th]
+        xn[1, start : start + size] = scaled.T[start : start + size]
+
+    def forward(g):
+        to_near[g].wait_recv()
+        to_core[g].start()
 
     part_sends, d_sends = {}, {}
-    for h in range(HALVES):
-        if h > 0:
-
-            @pl.when(half != i)
-            def _(h=h):
-                x_relay[h].wait_recv()
-                core_second[h].start()
-                y_first[h].wait_recv()
-                core_first[h].start()
-                y_own[0].wait_recv()
-                y_own[1].wait_recv()
-                core_own.start()
-
-        received(landed.at[h, pl.ds(0, flat)], core_recv.at[h])
-        unfold(h)
+    forward(0)
+
+    @pl.when(half == i)
+    def _():
+        y_own.start()
+
+    for g, (start, size) in enumerate(SENT_GROUPS):
+        to_core[g].wait_recv()
+        unfold(g)
+        these = pl.ds(start, size)
         for k in range(CHUNKS):
-            if h == 0:
-                for load in loads[k]:
-                    load.wait()
-            part_send[h, k] = jnp.dot(
-                xn[1, h * th : (h + 1) * th], w[k], preferred_element_type=f32
+            part_send[k, these] = jnp.dot(
+                xn[1, start : start + size], w[k], preferred_element_type=f32
             ).astype(bf)
-            copy = send(part_send.at[h, k], part_recv.at[h, k], part_ssem, part_rsem.at[h, k], xdev)
+            copy = send(part_send.at[k, these], part_recv.at[k, these], part_ssem, part_rsem.at[g, k], xdev)
             copy.start()
-            part_sends[h, k] = copy
+            part_sends[g, k] = copy
+            if k == 0 and g < n_sent - 1:
+                forward(g + 1)
+            if k == 1 and g == n_sent - 1:
+
+                @pl.when(half != i)
+                def _():
+                    y_own.wait_recv()
+                    core_own.start()
 
     @pl.when(s == t)
     def _():
@@ -363,14 +349,21 @@
     inv_all = jnp.broadcast_to(inv_row, (per_device, per_device)).T[:, :1]
     back_load.wait()
 
+    def send_d(r, k):
+        start, size = LATE_GROUPS[r]
+        these = pl.ds(start, size)
+        copy = send(d_all.at[0, k, these], d_all.at[1, k, these], d_ssem, d_rsem.at[r, k], xdev)
+        copy.start()
+        d_sends[r, k] = copy
+
     row_cols = []
-    for h in range(HALVES):
-        here = slice(h * th, (h + 1) * th)
+    for g, (start, size) in enumerate(SENT_GROUPS):
+        here = slice(start, start + size)
         inv = inv_all[here]
-        row_col = jnp.zeros((th, 1), f32)
+        row_col = jnp.zeros((size, 1), f32)
         for k in range(CHUNKS):
-            part_sends[h, k].wait_recv()
-            raw_sums = own_part[k, here] + part_recv[h, k].astype(f32)
+            part_sends[g, k].wait_recv()
+            raw_sums = own_part[k, here] + part_recv[k, here].astype(f32)
             gate, up = raw_sums[:, :ck] * inv, raw_sums[:, ck:] * inv
             grad = back[here, k * ck : (k + 1) * ck].astype(f32) * inv
             square = gate * gate
@@ -380,13 +373,13 @@
             d_gate, d_up = grad * up * slope, grad * gate * cdf
             d_all[0, k, here, pl.ds(0, ck)] = d_gate.astype(bf)
             d_all[0, k, here, pl.ds(ck, ck)] = d_up.astype(bf)
-            these = pl.ds(h * th, th)
-            copy = send(d_all.at[0, k, these], d_all.at[1, k, these], d_ssem, d_rsem.at[h, k], xdev)
-            copy.start()
-            d_sends[h, k] = copy
+            if g > 0:
+                send_d(g - 1, k)
             terms = d_gate * raw_sums[:, :ck] + d_up * raw_sums[:, ck:]
             row_col = row_col + jnp.sum(terms, axis=1, keepdims=True)
         row_cols.append(row_col)
+    for k in range(CHUNKS):
+        send_d(n_late - 1, k)
 
     row_col = jnp.concatenate(row_cols, axis=0)
     rows[0] = jnp.broadcast_to(row_col, (per_device, per_device)).T[:8]
@@ -435,17 +428,34 @@
             result = result + landing[slot].astype(f32)
         return result
 
-    acc = None
-    for k in range(CHUNKS):
-        term = lax.dot_general(w[k], d_all[0, k], CONTRACT_COLS, preferred_element_type=f32)
-        acc = term if acc is None else acc + term
+    def d_normed(slot, start, size):
+        total = None
+        for k in range(CHUNKS):
+            if slot == 1:
+                d_sends[late_of[start], k].wait_recv()
+            term = jnp.dot(d_all[slot, k, start : start + size], w_t[k], preferred_element_type=f32)
+            total = term if total is None else total + term
+            if slot == 1 and k == 0:
+                finish(late_of[start] - 1)
+        repeated = [total] * (per_device // size)
+        return (jnp.concatenate(repeated, axis=0) if len(repeated) > 1 else total).T
+
+    late_of = {start: r for r, (start, _) in enumerate(LATE_GROUPS)}
+    turned = d_normed(0, 0, per_device)
     for r in range(8):
-        own_pieces[r % 2, r // 2] = acc[r * own : (r + 1) * own].astype(bf)
-    own_swap = send(own_pieces.at[1 - q], own_sib, sib_ssem.at[HALVES], sib_rsem.at[HALVES], cdev)
-    own_swap.start()
-    own_swap.wait_recv()
-    own_halved[...] = (own_pieces[q].astype(f32) + own_sib[...].astype(f32)).astype(bf)
-    scatter(own_halved, own_incoming, HALVES)
+        own_pieces[r % 2, r // 2] = turned[r * own : (r + 1) * own].astype(bf)
+    swaps = {-1: send(own_pieces.at[1 - q], own_sib, sib_ssem.at[n_late], sib_rsem.at[n_late], cdev)}
+    swaps[-1].start()
+
+    def finish(r):
+        swaps[r].wait_recv()
+        if r < 0:
+            own_halved[...] = (own_pieces[q].astype(f32) + own_sib[...].astype(f32)).astype(bf)
+            scatter(own_halved, own_incoming, n_late)
+        else:
+            pieces, sib_in, halved, incoming, _, _ = late_bufs[r]
+            halved[...] = (pieces[q].astype(f32) + sib_in[...].astype(f32)).astype(bf)
+            scatter(halved, incoming, r)
 
     def weight_grads(k):
         both = jnp.concatenate([d_all[0, k], d_all[1, k]], axis=0)
@@ -454,30 +464,23 @@
         grad_gate[:, cols] = grads[:, :ck]
         grad_up[:, cols] = grads[:, ck:]
 
-    swaps = []
-    for h in range(HALVES):
-        acc = None
-        for k in range(CHUNKS):
-            d_sends[h, k].wait_recv()
-            late = d_all[1, k, h * th : (h + 1) * th]
-            twice = jnp.concatenate([late, late], axis=0)
-            term = lax.dot_general(w[k], twice, CONTRACT_COLS, preferred_element_type=f32)
-            acc = term if acc is None else acc + term
-            if h == HALVES - 1 and k == 0:
-                weight_grads(0)
-        for r in range(8):
-            top, bottom = acc[r * own : r * own + fold], acc[r * own + fold : (r + 1) * own]
-            pieces[h, r % 2, r // 2] = jnp.where(left_own, top, bottom).astype(bf)
-        swap = send(pieces.at[h, 1 - q], sib_in.at[h], sib_ssem.at[h], sib_rsem.at[h], cdev)
-        swap.start()
-        if h == HALVES - 1:
-            weight_grads(1)
-        swap.wait_recv()
-        swaps.append(swap)
-        halved[h] = (pieces[h, q].astype(f32) + sib_in[h].astype(f32)).astype(bf)
-        scatter(halved.at[h], incoming.at[h], h)
-
-    weight_grads(CHUNKS - 1)
+    def padded(value, height):
+        short = height - value.shape[0]
+        return jnp.concatenate([value, jnp.zeros((short, per_device), f32)], axis=0) if short else value
+
+    for r, (start, size) in enumerate(LATE_GROUPS):
+        turned = d_normed(1, start, size)
+        pieces, sib_in = late_bufs[r][:2]
+        cuts = spans(own, per_device // size)
+        for p in range(8):
+            parts = [padded(turned[p * own + at : p * own + at + n], cuts[0][1]) for at, n in cuts]
+            pieces[p % 2, p // 2] = pick(parts, size).astype(bf)
+        swaps[r] = send(pieces.at[1 - q], sib_in, sib_ssem.at[r], sib_rsem.at[r], cdev)
+        swaps[r].start()
+    weight_grads(0)
+    finish(n_late - 1)
+    for k in range(1, CHUNKS):
+        weight_grads(k)
     received(rows.at[pl.ds(1, 15)], row_sem.at[1])
     row_sum = rows[0]
     for slot in range(1, 16):
@@ -491,31 +494,28 @@
     mine = slab[...].astype(f32)
     gain_own = gain_col[pl.ds(pl.multiple_of((t * 4 + s) * own, 16), own)]
 
-    def moves(h):
-        return send(move_send.at[h], moved.at[h], last_send.at[0], last_recv.at[h], xdev)
-
-    gain_copy = send(gains.at[0], gains.at[1], last_send.at[1], last_recv.at[HALVES], xdev)
+    def moves(r):
+        return send(late_bufs[r][4], late_bufs[r][5], last_send.at[r], last_recv.at[r], xdev)
+
+    gain_copy = send(gains.at[0], gains.at[1], last_send.at[n_late], last_recv.at[n_late], xdev)
 
     @pl.when(reducer)
     def _():
-        d_own = gathered(own_incoming, HALVES)
+        d_own = gathered(own_incoming, n_late)
         grad_t[...] = (gain_own * d_own - mine * factor).astype(bf)
         prods[pl.ds(0, own)] = mine * d_own
         prods[pl.ds(own, prods.shape[0] - own)] = jnp.zeros((prods.shape[0] - own, per_device), f32)
         local = pl.multiple_of((lax.rem(t, 2) * 4 + s) * own, 16)
         theirs = xg[1, pl.ds(local, own)].astype(f32)
-        top, bottom = theirs[:fold], theirs[fold:]
-        for h in range(HALVES):
-            d_late = gathered(incoming.at[h], h)
-            move_send[h] = d_late.astype(bf)
-            moves(h).start()
-            if h == 0:
-                match = jnp.where(left_own, top, pltpu.roll(bottom, th, 1))
-            else:
-                match = jnp.where(left_own, pltpu.roll(top, th, 1), bottom)
-            product = d_late * match
-            prods[pl.ds(0, fold)] += jnp.where(left_own, product, 0.0)
-            prods[pl.ds(fold, fold)] += jnp.where(left_own, 0.0, product)
+        for r, (start, size) in enumerate(LATE_GROUPS):
+            d_late = gathered(late_bufs[r][3], r)
+            late_bufs[r][4][...] = d_late.astype(bf)
+            moves(r).start()
+            cuts = spans(own, per_device // size)
+            for j, (at, n) in enumerate(cuts):
+                product = d_late[:n] * turn(theirs[at : at + n], j * size - start)
+                inside = (lane >= j * size) & (lane < (j + 1) * size)
+                prods[pl.ds(at, n)] += jnp.where(inside, product, 0.0)
         gains[0] = jnp.broadcast_to(jnp.sum(prods[...].T, axis=0, keepdims=True), gains.shape[1:])
         gain_copy.start()
         gain_out[...] = gains[0, :1, :own]
@@ -523,16 +523,14 @@
     def drain():
         @pl.when(half != i)
         def _():
-            sent(folded, tok_send.at[0])
-            sent(relay, tok_send.at[1])
+            sent(x_in, tok_send.at[0])
+            sent(x_in, tok_send.at[1])
 
         @pl.when(half == i)
         def _():
             sent(x_in, tok_send.at[0])
-            sent(relay, tok_send.at[1])
-            sent(relay, tok_send.at[2])
-
-        sent(folded, core_send.at[0])
+
+        sent(x_in, core_send.at[0])
         sent(x_in, core_send.at[1])
 
         @pl.when(s == t)
@@ -543,27 +541,31 @@
         sent(part_send, part_ssem)
         sent(d_all.at[0], d_ssem)
         sent(rows.at[pl.ds(1, 15)], row_sem.at[0])
-        for copy in [own_swap] + swaps:
+        for copy in swaps.values():
             copy.wait_send()
-        scattered(own_halved, HALVES)
-        for h in range(HALVES):
-            scattered(halved.at[h], h)
+        scattered(own_halved, n_late)
+        for r in range(n_late):
+            scattered(late_bufs[r][2], r)
 
     drain()
 
     @pl.when(reducer)
     def _():
-        sent(move_send, last_send.at[0])
+        for r in range(n_late):
+            moves(r).wait_send()
         gain_copy.wait_send()
 
     @pl.when(not_reducer)
     def _():
-        moves(0).wait_recv()
-        moves(1).wait_recv()
-        early, final = moved[0].astype(f32), moved[1].astype(f32)
-        top = jnp.where(left_own, early, pltpu.roll(final, th, 1))
-        bottom = jnp.where(left_own, pltpu.roll(early, th, 1), final)
-        grad_t[...] = (gain_own * jnp.concatenate([top, bottom], axis=0) - mine * factor).astype(bf)
+        d_own = None
+        for r, (start, size) in enumerate(LATE_GROUPS):
+            moves(r).wait_recv()
+            value = late_bufs[r][5][...].astype(f32)
+            cuts = spans(own, per_device // size)
+            turned = [turn(value[:n], start - j * size) for j, (at, n) in enumerate(cuts)]
+            part = jnp.concatenate(turned, axis=0)
+            d_own = part if d_own is None else jnp.where(lane >= start, part, d_own)
+        grad_t[...] = (gain_own * d_own - mine * factor).astype(bf)
         gain_copy.wait_recv()
         gain_out[...] = gains[1, :1, :own]
 
@@ -590,9 +592,6 @@
     full = norm_gain.shape[0]
     own = full // 16
     ck = width // CHUNKS
-    th = per_device // HALVES
-    fold = own // 2
-    flat = sec_rows // 2
     bf, f32 = jnp.bfloat16, jnp.float32
     vmem = pl.BlockSpec(memory_space=pltpu.VMEM)
     anywhere = pl.BlockSpec(memory_space=pltpu.HBM)
@@ -604,6 +603,9 @@
         jax.ShapeDtypeStruct((block, width), bf),
         jax.ShapeDtypeStruct((block, width), bf),
     )
+    n_sent, n_late = len(SENT_GROUPS), len(LATE_GROUPS)
+    sent_rows = [sec_rows * size // per_device for _, size in SENT_GROUPS]
+    late_rows = [spans(own, per_device // size)[0][1] for _, size in LATE_GROUPS]
     operands = (tokens.T, norm_gain.reshape(full // 128, 128), hidden_grad, w_gate, w_up)
     results = pl.pallas_call(
         functools.partial(exchange_kernel, full),
@@ -612,57 +614,52 @@
         out_specs=(vmem,) * 4,
         scratch_shapes=[
             pltpu.VMEM((sec_rows, per_device), bf),
-            pltpu.VMEM((HALVES, flat, per_device), bf),
+            [pltpu.VMEM((n, per_device), bf) for n in sent_rows],
+            [pltpu.VMEM((2 * n, per_device), bf) for n in sent_rows],
             pltpu.VMEM((full // 128, 128), f32),
             pltpu.VMEM((full, 128), f32),
             pltpu.VMEM((CHUNKS, block, 2 * ck), bf),
+            pltpu.VMEM((CHUNKS, 2 * ck, block), bf),
             pltpu.VMEM((per_device, width), bf),
-            pltpu.VMEM((HALVES, flat // 2, per_device), bf),
-            pltpu.VMEM((HALVES, 2 * flat, per_device), bf),
             pltpu.VMEM((2, block, per_device), bf),
             pltpu.VMEM((block, 2 * per_device), bf),
             pltpu.VMEM((2, per_device, block), bf),
             pltpu.VMEM((own, per_device), bf),
             pltpu.VMEM((4, 8, per_device), f32),
-            pltpu.VMEM((HALVES, CHUNKS, th, 2 * ck), bf),
-            pltpu.VMEM((HALVES, CHUNKS, th, 2 * ck), bf),
+            pltpu.VMEM((CHUNKS, per_device, 2 * ck), bf),
+            pltpu.VMEM((CHUNKS, per_device, 2 * ck), bf),
             pltpu.VMEM((CHUNKS, per_device, 2 * ck), f32),
             pltpu.VMEM((2, CHUNKS, per_device, 2 * ck), bf),
             pltpu.VMEM((2, 4, own, per_device), bf),
             pltpu.VMEM((4, own, per_device), bf),
             pltpu.VMEM((4, own, per_device), bf),
             pltpu.VMEM((8, own, per_device), bf),
-            pltpu.VMEM((HALVES, 2, 4, fold, per_device), bf),
-            pltpu.VMEM((HALVES, 4, fold, per_device), bf),
-            pltpu.VMEM((HALVES, 4, fold, per_device), bf),
-            pltpu.VMEM((HALVES, 8, fold, per_device), bf),
-            pltpu.VMEM((HALVES, fold, per_device), bf),
-            pltpu.VMEM((HALVES, fold, per_device), bf),
+            [
+                [pltpu.VMEM((*lead, n, per_device), bf) for lead in ((2, 4), (4,), (4,), (8,), (), ())]
+                for n in late_rows
+            ],
             pltpu.VMEM((16, 8, per_device), f32),
             pltpu.VMEM((own_pad, per_device), f32),
             pltpu.VMEM((2, 8, own_pad), f32),
             pltpu.SemaphoreType.REGULAR((3,)),
             dma((3,)),
             dma((2, CHUNKS)),
-            dma((3,)),
-            dma((HALVES,)),
-            dma((HALVES,)),
-            dma((HALVES,)),
-            dma((HALVES,)),
             dma((2,)),
-            dma((HALVES + 1,)),
+            dma((n_sent + 1,)),
+            dma((2,)),
+            dma((n_sent + 1,)),
             dma((2,)),
             dma((2,)),
             dma,
-            dma((HALVES, CHUNKS)),
+            dma((n_sent, CHUNKS)),
             dma,
-            dma((HALVES, CHUNKS)),
-            dma((HALVES + 1,)),
-            dma((HALVES + 1,)),
-            dma((HALVES + 1,)),
-            dma((HALVES + 1,)),
-            dma((2,)),
-            dma((HALVES + 1,)),
+            dma((n_late, CHUNKS)),
+            dma((n_late + 1,)),
+            dma((n_late + 1,)),
+            dma((n_late + 1,)),
+            dma((n_late + 1,)),
+            dma((n_late + 1,)),
+            dma((n_late + 1,)),
             dma((2,)),
         ],
         compiler_params=pltpu.CompilerParams(

time: 53.2 us -> 49.5 us (0.930)
  Pallas kernels: 52.4 us -> 48.7 us
    pallas_call x1, Pallas kernels: 49.9 us -> 46.2 us  [fused_shards(): pl.pallas_call(functools.partial(exchange_kernel, full), out_shape=tuple(...]
where the time goes in v3:
time: 49.5 us; the launch traced here: 49.4 us
  Pallas kernels  48.7 us (98%)
  between operations  0.64 us (1%)
    pallas_call x1, Pallas kernels, fused_shards(): pl.pallas_call(functools.partial(exchange_kernel, full), out_shape=tuple(...  46.2 us
    pallas_call x1, Pallas kernels, fused_shards(): pl.pallas_call(write_kernel, out_shape=kept, in_specs=[vmem] * 4, out_spe...  2.47 us

profile of v3, /device:TPU:0, one launch (start us, length us, event | category | flops | bytes accessed | tf_op | source)
XLA Modules:
  0.0 49.4 jit_solution(6830492237282052687)
XLA Ops:
  0.6 46.2 %shard_map.84 = (bf16[144,128]{1,0:T(8,128)(2,1)S(1)}, f32[1,144]{1,0:T(1,128)S(1)}, bf16[1152,1152]{1,0:T(8,128)(2,1)S(1)}, bf16[1152,1152]{1,0:T(8,128)(2,1)S(1)}) custom-call(bf16[576,128]{1,0:T(8,128)(2,1)} %bitcast.4, f32[18,128]{1,0:T(8,128)} %bitcast.5, bf16[128,1152]{1,0:T(8,128)(2,1)} %back_hbm.1, bf16[1152,1152]{1,0:T(8,128)(2,1)} %wg_hbm.1, ...), custom_call_target="tpu_custom_call" | custom-call | tf_op jit(solution)/shard_map/pallas_call | solution.py:610
  46.9 2.5 %shard_map.85 = (bf16[144,128]{1,0:T(8,128)(2,1)}, f32[1,144]{1,0:T(1,128)}, bf16[1152,1152]{1,0:T(8,128)(2,1)}, bf16[1152,1152]{1,0:T(8,128)(2,1)}) custom-call(bf16[144,128]{1,0:T(8,128)(2,1)S(1)} %get-tuple-element.12.grad_t, f32[1,144]{1,0:T(1,128)S(1)} %get-tuple-element.13.gain, bf16[1152,1152]{1,0:T(8,128)(2,1)S(1)} %get-tuple-element.14.grad_gate, ...), custom_call_target="tpu_custom_call" | custom-call | tf_op jit(solution)/shard_map/pallas_call | solution.py:669
